TPU v7x, 256 devices: a whole 4x4x8 slice. The times are simulated.
256 devices in a mesh: cuts: 32 (over z, x), mode: 8 (over y, core).
Axes of the slice: x: 4, y: 4, z: 8, core: 2. Of those that a mesh axis runs over, the one named last changes fastest.
Arguments:
- sliced_state: bfloat16 [8, 64, 4, 128, 2, 128], P(None, 'cuts', None, 'mode'), may hold values from -0.75 to 0.75
- gate_blocks: bfloat16 [32, 2, 128, 128], P('cuts'), may hold values from -0.375 to 0.375
- gate_slot: int32 [32], replicated, may hold values from 0 to 31, each once
- samples: int32 [8, 4096], replicated, may hold values from 0 to 65535
Outputs:
- amplitudes: float32 [32, 128, 2, 128], P('cuts', 'mode')
- sample_probs: float32 [8, 4096], replicated
- xeb_score: float32 [8], replicated
Inputs may be any that keep to these rules, and one draw needn't show every extreme that they name: `gate_slot`: a permutation: every gate block has its own row of gate_blocks. `samples`: flat index s * 128 * 128 + p * 128 + q.
All inputs are finite; a program needn't handle non-finite values.
Results may differ from a plain program's by a relative error of at most 0.022.
Values may be sent and summed in bfloat16 or wider, within the bound.
No kernel may reach another device: no remote copies, remote signals or barrier semaphores. Data moves between devices by JAX's collectives and lax.ppermute only.
A program may use at most 64 MiB of HBM per device.

v0:
```python
import functools

import jax
import jax.numpy as jnp
from jax import lax
from jax.sharding import Mesh
from jax.sharding import PartitionSpec as P

MODE = ("mode_0", "mode_1")
CUTS = ("cuts_0", "cuts_1")
CUTS_MODE = ("cuts_0", "cuts_1", "mode_0", "mode_1")


def gathered_by_axis(array, axes, dim):
    if not axes:
        return array
    nearer = lax.all_gather(array, axes[-1], axis=dim, tiled=True)
    return gathered_by_axis(nearer, axes[:-1], dim)


def cut_along(array, dim, count):
    before, after = (array.shape[:dim], array.shape[dim + 1 :])
    return jnp.moveaxis(array.reshape(*before, count, -1, *after), dim, 0)


def sum_at_owner(array, axis, dim):
    tiles = cut_along(array, dim, lax.axis_size(axis))
    arrived = lax.all_to_all(tiles, axis, split_axis=0, concat_axis=0, tiled=True)
    return arrived.astype(jnp.float32).sum(axis=0)


def by_axis(array, axes):
    return functools.reduce(lax.psum, axes, array)


def apply_gates(tensor, blocks):
    real_part = blocks[:, 0]
    imag_part = blocks[:, 1]
    stacked = jnp.concatenate(
        [
            jnp.concatenate([real_part, imag_part], axis=2),
            jnp.concatenate([-imag_part, real_part], axis=2),
        ],
        axis=1,
    )
    layout = tensor.shape
    flattened = tensor.reshape(layout[0], -1, 2 * layout[-1])
    product = jnp.einsum("crk,ckn->crn", flattened, stacked, preferred_element_type=jnp.float32)
    return product.astype(jnp.bfloat16).reshape(layout)


def select_rows(table, wanted):
    count = table.shape[0]
    onehot = (wanted[:, None] == jnp.arange(count, dtype=jnp.int32)[None, :]).astype(table.dtype)
    picked = jnp.dot(onehot, table.reshape(count, -1), preferred_element_type=jnp.float32)
    return picked.astype(table.dtype).reshape((wanted.shape[0],) + table.shape[1:])


def on_device(sliced_state, gate_blocks, gate_slot, samples):
    circuits = sliced_state.shape[0]
    spectator = sliced_state.shape[2]
    width = sliced_state.shape[5]
    layer_count = gate_slot.shape[0] // (2 * circuits)
    circuit_ids = jnp.arange(circuits, dtype=jnp.int32)
    tensor = lax.all_to_all(sliced_state, MODE, split_axis=0, concat_axis=3, tiled=True)
    local_count = tensor.shape[0]
    local_ids = lax.axis_index(MODE) * local_count + jnp.arange(local_count, dtype=jnp.int32)
    gathered = gathered_by_axis(gate_blocks, CUTS, 0)

    def fetch_gates(layer_index, gate_kind):
        return select_rows(
            gathered, gate_slot[(local_ids * layer_count + layer_index) * 2 + gate_kind]
        )

    for layer_index in range(layer_count):
        tensor = apply_gates(tensor, fetch_gates(layer_index, 0))
        tensor = jnp.swapaxes(tensor, 3, 5)
        tensor = apply_gates(tensor, fetch_gates(layer_index, 1))
        tensor = jnp.swapaxes(tensor, 3, 5)
    summed = jnp.sum(tensor.astype(jnp.float32), axis=1)
    summed = lax.all_to_all(
        summed.astype(jnp.bfloat16), MODE, split_axis=2, concat_axis=0, tiled=True
    ).astype(summed.dtype)
    local_rows = summed.shape[2]
    summed = summed.reshape(circuits * spectator, local_rows, 2, width)
    amplitudes = sum_at_owner(summed.astype(jnp.bfloat16), CUTS, 0)
    row_count = amplitudes.shape[0]
    first_row = lax.axis_index(CUTS) * row_count
    first_col = lax.axis_index(MODE) * local_rows
    magnitude = amplitudes[:, :, 0, :] ** 2 + amplitudes[:, :, 1, :] ** 2
    row_sums = jnp.sum(magnitude, axis=(1, 2))
    owner_circuit = (first_row + jnp.arange(row_count, dtype=jnp.int32)) // spectator
    norm_part = jnp.sum(
        jnp.where(owner_circuit[None, :] == circuit_ids[:, None], row_sums[None, :], 0.0), axis=1
    )
    plane_size = width * width
    spec_index = samples // plane_size
    row_index = samples // width % width
    col_index = samples % width
    local_row = circuit_ids[:, None] * spectator + spec_index - first_row
    local_col = row_index - first_col
    is_owned = (
        (local_row >= 0) & (local_row < row_count) & (local_col >= 0) & (local_col < local_rows)
    )
    cell_index = jnp.where(is_owned, local_row * local_rows + local_col, -1)
    cell_count = row_count * local_rows
    cell_onehot = (
        cell_index[:, :, None] == jnp.arange(cell_count, dtype=jnp.int32)[None, None, :]
    ).astype(jnp.float32)
    picked_rows = jnp.einsum("csr,rw->csw", cell_onehot, magnitude.reshape(cell_count, width))
    col_match = col_index[:, :, None] == jnp.arange(width, dtype=jnp.int32)[None, None, :]
    sample_mass = jnp.sum(jnp.where(col_match, picked_rows, 0.0), axis=2)
    dimension_scale = float(spectator * plane_size)
    mass_total, norm_total = (by_axis(sample_mass, CUTS_MODE), by_axis(norm_part, CUTS_MODE))
    sample_probs = mass_total * dimension_scale / norm_total[:, None]
    xeb_score = jnp.mean(sample_probs, axis=1)
    return (amplitudes, sample_probs, xeb_score)


def solution(mesh):
    split = Mesh(mesh.devices.reshape(8, 4, 4, 2), ("cuts_0", "cuts_1", "mode_0", "mode_1"))
    placed = (P(None, CUTS, None, MODE, None, None), P(CUTS, None, None, None), P(), P())
    return jax.shard_map(
        on_device,
        mesh=split,
        in_specs=placed,
        out_specs=(P(CUTS, MODE, None, None), P(), P()),
        check_vma=False,
    )
```

profile of v0, /device:TPU:1, one launch (start us, length us, event | category | flops | bytes accessed | tf_op | source)
XLA Modules:
  0.0 329.6 jit_solution(11438945458227351211)
XLA Ops:
  7.2 12.4 %all_gather.6 = bf16[4,2,128,128]{3,2,1,0:T(8,128)(2,1)} all-gather(bf16[1,2,128,128]{3,2,1,0:T(8,128)(2,1)} %param.5), channel_id=1, replica_groups=mesh['cuts_0'=8,'cuts_1'=4,'mode_0'=4,'mode_1'=2] {'cuts_1'}, dimensions={0}, use_global_device_ids=true | all-gather | bytes 327680 | tf_op jit(solution)/shard_map/all_gather | solution.py:17
  19.6 7.8 %all-to-all-start = ((bf16[8,2,4,16,2,128]{5,4,3,2,1,0:T(2,128)(2,1)}), bf16[8,2,4,16,2,128]{5,4,3,2,1,0:T(2,128)(2,1)S(1)}, u32[]{:S(2)}, u32[]{:S(2)}) async-start(bf16[8,2,4,16,2,128]{5,4,3,2,1,0:T(2,128)(2,1)} %param.4), calls=%async_computation | async-start | bytes 1048576 | tf_op jit(solution)/shard_map/all_to_all | solution.py:65
  27.4 1.5 fusion.82
  28.9 7.9 %all-to-all-done = bf16[8,2,4,16,2,128]{5,4,3,2,1,0:T(2,128)(2,1)S(1)} async-done(((bf16[8,2,4,16,2,128]{5,4,3,2,1,0:T(2,128)(2,1)}), bf16[8,2,4,16,2,128]{5,4,3,2,1,0:T(2,128)(2,1)S(1)}, u32[]{:S(2)}, u32[]{:S(2)}) %all-to-all-start) | async-done | bytes 524320 | tf_op jit(solution)/shard_map/all_to_all | solution.py:65
  37.2 23.6 %all-gather.2.cloned.1.call-done = bf16[32,2,128,128]{3,2,1,0:T(8,128)(2,1)} async-done(((bf16[4,2,128,128]{3,2,1,0:T(8,128)(2,1)}), bf16[32,2,128,128]{3,2,1,0:T(8,128)(2,1)}) %all-gather.2.cloned.1.call-update) | async-done | bytes 2097168 | tf_op jit(solution)/shard_map/all_gather | solution.py:17
  60.8 3.6 %fusion.6 = f32[1,32768]{1,0:T(1,128)S(1)} fusion(bf16[4,8,256,128]{3,2,1,0:T(8,128)(2,1)} %bitcast.126, s32[]{:T(128)} %bitcast.2), kind=kOutput, calls=%fused_computation.8 | convolution fusion | flops 2097184 | bytes 2228228 | tf_op jit(solution)/shard_map/dot_general | solution.py:55
  64.4 1.9 fusion.4
  66.3 1.9 fusion.2
  68.3 1.8 fusion
  70.9 0.5 copy.13
  71.8 0.6 copy.14
  72.9 0.6 copy.15
  74.0 1.2 reduce_sum.58
  75.2 1.0 copy.16
  76.2 9.2 %all-to-all-start.1 = ((bf16[1,4,128,2,128]{4,3,1,0,2:T(2,128)(2,1)}), bf16[1,4,128,2,128]{4,3,1,0,2:T(2,128)(2,1)S(1)}, u32[]{:S(2)}, u32[]{:S(2)}) async-start(bf16[1,4,128,2,128]{4,3,1,0,2:T(2,128)(2,1)} %copy.16), calls=%async_computation.1 | async-start | bytes 524288 | tf_op jit(solution)/shard_map/all_to_all | solution.py:81
  85.3 6.5 %all-to-all-done.1 = bf16[1,4,128,2,128]{4,3,1,0,2:T(2,128)(2,1)S(1)} async-done(((bf16[1,4,128,2,128]{4,3,1,0,2:T(2,128)(2,1)}), bf16[1,4,128,2,128]{4,3,1,0,2:T(2,128)(2,1)S(1)}, u32[]{:S(2)}, u32[]{:S(2)}) %all-to-all-start.1) | async-done | bytes 262176 | tf_op jit(solution)/shard_map/all_to_all | solution.py:81
  91.9 0.7 copy.18
  92.6 6.8 %all-to-all-start.2 = ((bf16[32,1,16,2,128]{4,2,3,1,0:T(8,128)(2,1)}), bf16[32,1,16,2,128]{4,2,3,1,0:T(8,128)(2,1)S(1)}, u32[]{:S(2)}, u32[]{:S(2)}) async-start(bf16[32,1,16,2,128]{4,2,3,1,0:T(8,128)(2,1)} %bitcast.48), calls=%async_computation.2 | async-start | bytes 524288 | tf_op jit(solution)/shard_map/all_to_all | solution.py:28
  99.9 10.1 %all-to-all-done.2 = bf16[32,1,16,2,128]{4,2,3,1,0:T(8,128)(2,1)S(1)} async-done(((bf16[32,1,16,2,128]{4,2,3,1,0:T(8,128)(2,1)}), bf16[32,1,16,2,128]{4,2,3,1,0:T(8,128)(2,1)S(1)}, u32[]{:S(2)}, u32[]{:S(2)}) %all-to-all-start.2) | async-done | bytes 262176 | tf_op jit(solution)/shard_map/all_to_all | solution.py:28
  110.1 3.6 %select_reduce_fusion = f32[8,4096]{1,0:T(8,128)} fusion(s32[8,4096]{1,0:T(8,128)S(1)} %get-tuple-element.53, s32[8,4096]{1,0:T(8,128)S(1)} %get-tuple-element.52, f32[1,16,2,128]{3,1,2,0:T(8,128)S(1)} %bitcast.149), kind=kOutput, calls=%fused_computation | convolution fusion | flops 147298304 | bytes 409600 | tf_op jit(solution)/shard_map/csr,rw->csw/dot_general | solution.py:110
  113.7 63.6 %all-reduce.5.cloned.1.call-done = f32[8,4096]{1,0:T(8,128)} async-done(((f32[8,4096]{1,0:T(8,128)}), f32[8,4096]{1,0:T(8,128)}) %all-reduce.5.cloned.1.call-update) | async-done | bytes 131088 | tf_op jit(solution)/shard_map/psum | solution.py:33
  177.4 50.2 %all-reduce.7.cloned.1.call-done = f32[8,4096]{1,0:T(8,128)} async-done(((f32[8,4096]{1,0:T(8,128)}), f32[8,4096]{1,0:T(8,128)}) %all-reduce.7.cloned.1.call-update) | async-done | bytes 131088 | tf_op jit(solution)/shard_map/psum | solution.py:33
  227.8 49.1 %all-reduce.9.cloned.1.call-done = f32[8,4096]{1,0:T(8,128)} async-done(((f32[8,4096]{1,0:T(8,128)}), f32[8,4096]{1,0:T(8,128)}) %all-reduce.9.cloned.1.call-update) | async-done | bytes 131088 | tf_op jit(solution)/shard_map/psum | solution.py:33
  276.9 0.6 fusion.63
  277.5 0.6 compare_select_fusion
  278.2 13.7 %psum.60 = f32[8]{0:T(128)S(1)} all-reduce(f32[8]{0:T(128)S(1)} %compare_select_fusion), channel_id=1, replica_groups=mesh['cuts_0'=8,'cuts_1'=4,'mode_0'=4,'mode_1'=2] {'cuts_0'}, use_global_device_ids=true, to_apply=%region_8.9 | all-reduce | flops 8 | bytes 64 | tf_op jit(solution)/shard_map/psum | solution.py:33
  291.9 8.4 %psum.61 = f32[8]{0:T(128)S(1)} all-reduce(f32[8]{0:T(128)S(1)} %psum.60), channel_id=1, replica_groups=mesh['cuts_0'=8,'cuts_1'=4,'mode_0'=4,'mode_1'=2] {'cuts_1'}, use_global_device_ids=true, to_apply=%region_9.10 | all-reduce | flops 8 | bytes 64 | tf_op jit(solution)/shard_map/psum | solution.py:33
  300.3 7.4 %psum.62 = f32[8]{0:T(128)S(1)} all-reduce(f32[8]{0:T(128)S(1)} %psum.61), channel_id=1, replica_groups=mesh['cuts_0'=8,'cuts_1'=4,'mode_0'=4,'mode_1'=2] {'mode_0'}, use_global_device_ids=true, to_apply=%region_10.11 | all-reduce | flops 8 | bytes 64 | tf_op jit(solution)/shard_map/psum | solution.py:33
  307.6 12.5 %psum.63 = f32[8]{0:T(128)S(1)} all-reduce(f32[8]{0:T(128)S(1)} %psum.62), channel_id=1, replica_groups=mesh['cuts_0'=8,'cuts_1'=4,'mode_0'=4,'mode_1'=2] {'mode_1'}, use_global_device_ids=true, to_apply=%region_11.12 | all-reduce | flops 8 | bytes 64 | tf_op jit(solution)/shard_map/psum | solution.py:33
  320.2 0.6 copy.19
  320.8 1.8 fusion.81
  322.5 0.5 broadcast_multiply_fusion
  (40 shorter events, 3.3 us)
Async XLA Ops:
  7.2 53.6 %all-gather.2.cloned.1.call-start = ((), (), s32[]{:S(2)}) async-start(), calls=%async_computation.3 | async-start | bytes 2359296 | tf_op jit(solution)/shard_map/all_gather | solution.py:17
  19.6 17.1 %all-to-all-start = ((bf16[8,2,4,16,2,128]{5,4,3,2,1,0:T(2,128)(2,1)}), bf16[8,2,4,16,2,128]{5,4,3,2,1,0:T(2,128)(2,1)S(1)}, u32[]{:S(2)}, u32[]{:S(2)}) async-start(bf16[8,2,4,16,2,128]{5,4,3,2,1,0:T(2,128)(2,1)} %param.4), calls=%async_computation | async-start | bytes 1048576 | tf_op jit(solution)/shard_map/all_to_all | solution.py:65
  60.8 3.6 %copy-start = (bf16[32,2,128,128]{3,2,1,0:T(8,128)(2,1)S(1)}, bf16[32,2,128,128]{3,2,1,0:T(8,128)(2,1)}, u32[]{:S(2)}) copy-start(bf16[32,2,128,128]{3,2,1,0:T(8,128)(2,1)} %all-gather.2.cloned.1.call-done) | copy-start | bytes 6291460
  73.8 25.8 %copy-start.1 = (s32[8,4096]{1,0:T(8,128)S(1)}, s32[8,4096]{1,0:T(8,128)}, u32[]{:S(2)}) copy-start(s32[8,4096]{1,0:T(8,128)} %param.7) | copy-start | bytes 393220
  76.2 15.6 %all-to-all-start.1 = ((bf16[1,4,128,2,128]{4,3,1,0,2:T(2,128)(2,1)}), bf16[1,4,128,2,128]{4,3,1,0,2:T(2,128)(2,1)S(1)}, u32[]{:S(2)}, u32[]{:S(2)}) async-start(bf16[1,4,128,2,128]{4,3,1,0,2:T(2,128)(2,1)} %copy.16), calls=%async_computation.1 | async-start | bytes 524288 | tf_op jit(solution)/shard_map/all_to_all | solution.py:81
  92.6 17.5 %all-to-all-start.2 = ((bf16[32,1,16,2,128]{4,2,3,1,0:T(8,128)(2,1)}), bf16[32,1,16,2,128]{4,2,3,1,0:T(8,128)(2,1)S(1)}, u32[]{:S(2)}, u32[]{:S(2)}) async-start(bf16[32,1,16,2,128]{4,2,3,1,0:T(8,128)(2,1)} %bitcast.48), calls=%async_computation.2 | async-start | bytes 524288 | tf_op jit(solution)/shard_map/all_to_all | solution.py:28
  99.4 78.0 %all-reduce.5.cloned.1.call-start = ((), (), s32[]{:S(2)}) async-start(), calls=%async_computation.4 | async-start | bytes 262144 | tf_op jit(solution)/shard_map/psum | solution.py:33
  113.7 114.0 %all-reduce.7.cloned.1.call-start = ((), (), s32[]{:S(2)}) async-start(), calls=%async_computation.5 | async-start | bytes 262144 | tf_op jit(solution)/shard_map/psum | solution.py:33
  177.4 99.5 %all-reduce.9.cloned.1.call-start = ((), (), s32[]{:S(2)}) async-start(), calls=%async_computation.6 | async-start | bytes 262144 | tf_op jit(solution)/shard_map/psum | solution.py:33
  227.7 93.1 %all-reduce.11.cloned.1.call-start = ((), (), s32[]{:S(2)}) async-start(), calls=%async_computation.7 | async-start | bytes 262144 | tf_op jit(solution)/shard_map/psum | solution.py:33
Sparse Core Ops, SparseCore 0:
  19.8 40.9 all-gather.1
  113.8 63.5 all-reduce.4
  179.7 47.9 all-reduce.6
  229.8 47.0 all-reduce.8
  279.3 31.9 all-reduce.10
where the time goes:
time: 330 us
  waiting for transfers between devices  211 us (64%)
  blocking collectives  54.4 us (16%)
  starting transfers between devices  24.1 us (7%)
  matrix products  14 us (4%)
  between operations  14 us (4%)
  local copies, waits for them, and re-layouts  6.8 us (2%)
  other arithmetic  5.13 us (2%)
    psum x4, waiting for transfers between devices, by_axis(): return functools.reduce(lax.psum, axes, array)  163 us
    psum x4, blocking collectives, by_axis(): return functools.reduce(lax.psum, axes, array)  42 us
    all_gather x1, waiting for transfers between devices, gathered_by_axis(): nearer = lax.all_gather(array, axes[-1], axis=dim, tiled=True)  23.6 us
    all_gather x1, blocking collectives, gathered_by_axis(): nearer = lax.all_gather(array, axes[-1], axis=dim, tiled=True)  12.4 us
    all_to_all x1, waiting for transfers between devices, sum_at_owner(): lax.all_to_all(tiles, axis, split_axis=0, concat_axis=0, tiled=True)  10.1 us
    dot_general x4, matrix products, select_rows(): jnp.dot(onehot, table.reshape(count, -1), preferred_element_type=jnp.floa...  9.17 us
    all_to_all x1, starting transfers between devices, on_device(): lax.all_to_all(summed.astype(jnp.bfloat16), MODE, split_axis=2, concat_ax...  9.15 us
    all_to_all x1, waiting for transfers between devices, on_device(): lax.all_to_all(sliced_state, MODE, split_axis=0, concat_axis=3, tiled=True)  7.88 us
  transfers between devices with their start and end apart: 8, of which 7 were waited for; matrix products, arithmetic and copies ran while one was open for 1% of the time, Pallas kernels for 0%

commit v1 on v0

v1 whole, which is shorter than its diff:
```python
import functools

import jax
import jax.numpy as jnp
from jax import lax
from jax.experimental import pallas as pl
from jax.experimental.pallas import tpu as pltpu
from jax.sharding import Mesh
from jax.sharding import PartitionSpec as P

BF, F32, I32 = jnp.bfloat16, jnp.float32, jnp.int32
Z, X, Y, K = 8, 4, 4, 2
M = Y * K
W = 128
VM = pl.BlockSpec(memory_space=pltpu.VMEM)
SM = pl.BlockSpec(memory_space=pltpu.SMEM)


def mode_index():
    return lax.axis_index("y") * K + lax.axis_index("k")


def dot(a, b):
    return jnp.dot(a, b, preferred_element_type=F32)


def pack_kernel(state_ref, gates_ref, out_ref):
    mode = mode_index()
    for c in range(Z):
        for s in range(X):
            total = state_ref[c, 0, s].astype(F32) + state_ref[c, 1, s].astype(F32)
            out_ref[c * X + s, 0:32, :] = total.astype(BF)
    for s in range(X):
        start = pl.multiple_of((s * M + mode) * 8, 8)
        rows = gates_ref[pl.ds(start, 8), :]
        for c in range(Z):
            out_ref[c * X + s, 32:40, :] = rows


def sum_kernel(slot_ref, in_ref, out_ref, sum_ref):
    circuit = lax.axis_index("z")
    total = in_ref[0, 0:32, :].astype(F32)
    for i in range(1, Z * X):
        total = total + in_ref[i, 0:32, :].astype(F32)
    sum_ref[...] = total
    state = jnp.concatenate([sum_ref[pl.ds(0, 16, stride=2), :], sum_ref[pl.ds(1, 16, stride=2), :]], axis=0).astype(BF)
    gates = [in_ref[slot_ref[circuit * 4 + b], 32:40, :] for b in range(4)]
    for i in range(X * M):
        out_ref[i, 0:32, :] = state
        for b in range(4):
            out_ref[i, 32 + 8 * b : 40 + 8 * b, :] = gates[b]


def embed(real, imag):
    return jnp.concatenate([jnp.concatenate([real, imag], axis=1), jnp.concatenate([-imag, real], axis=1)], axis=0)


def compose(first, second):
    left = jnp.concatenate([first[:W], first[W:]], axis=1)
    return dot(left, embed(second[:W], second[W:]))


def apply_kernel(samples_ref, in_ref, amp_ref, out_ref, full_ref, pick_ref):
    circuit = lax.axis_index("z")
    spect = lax.axis_index("x")
    mode = mode_index()
    g = [in_ref[:, 32 + 8 * b : 40 + 8 * b, :].reshape(2 * W, W) for b in range(4)]
    col = compose(g[0], g[2]).astype(BF)
    row = compose(g[1], g[3])
    row_r, row_i = row[:, :W].T.astype(BF), row[:, W:].T.astype(BF)
    gate_q = embed(col[:, :W], col[:, W:])
    gate_p = jnp.concatenate([jnp.concatenate([row_r, -row_i], axis=1), jnp.concatenate([row_i, row_r], axis=1)], axis=0)
    real = in_ref[:, 0:16, :].reshape(X * W, W)
    imag = in_ref[:, 16:32, :].reshape(X * W, W)
    mid = dot(jnp.concatenate([real, imag], axis=1), gate_q).astype(BF)
    mid = jnp.concatenate(
        [jnp.concatenate([mid[s * W : (s + 1) * W, r * W : (r + 1) * W] for s in range(X)], axis=1) for r in range(2)], axis=0
    )
    full = dot(gate_p, mid)
    for s in range(X):
        for r in range(2):
            full_ref[s, r] = full[r * W : (r + 1) * W, s * W : (s + 1) * W]
    start = pl.multiple_of(mode * 16, 16)
    for r in range(2):
        amp_ref[0, :, r, :] = full_ref[spect, r, pl.ds(start, 16), :]
    mag = full[:W] * full[:W] + full[W:] * full[W:]
    norm = jnp.sum(mag)
    table = jnp.concatenate([mag[:, : 2 * W], mag[:, 2 * W :]], axis=0).astype(BF)
    chunk = 512
    for j in range(4096 // chunk):
        flat = samples_ref[pl.ds(circuit, 1), j * chunk : (j + 1) * chunk]
        lane = ((flat >> 14) & 1) * W + (flat & 127)
        line = ((flat >> 15) & 1) * W + ((flat >> 7) & 127)
        ids = lax.broadcasted_iota(I32, (2 * W, chunk), 0)
        onehot = jnp.where(ids == lane, 1.0, 0.0).astype(BF)
        got = dot(table, onehot)
        got = jnp.sum(jnp.where(ids == line, got, 0.0), axis=0, keepdims=True)
        for i in range(chunk // W):
            pick_ref[j * (chunk // W) + i : j * (chunk // W) + i + 1, :] = got[:, i * W : (i + 1) * W]
    picked = pick_ref[...].astype(BF)
    tail = jnp.full((8, W), norm, F32)
    high = tail.astype(BF).astype(F32)
    tail = jnp.where(lax.broadcasted_iota(I32, (8, W), 0) == 0, high, tail - high).astype(BF)
    for c in range(Z):
        out_ref[c, 0:32, :] = picked
        out_ref[c, 32:40, :] = tail


def finish_kernel(in_ref, probs_ref, score_ref, wide_ref):
    for c in range(Z):
        tail = in_ref[c, 32:40, :].astype(F32)
        norm = tail[0:1] + tail[1:2]
        wide_ref[c * 32 : (c + 1) * 32, :] = in_ref[c, 0:32, :].astype(F32) * 65536.0 / norm
    total = jnp.zeros((Z, W), F32)
    for j in range(32):
        rows = wide_ref[pl.ds(j, Z, stride=32), :]
        probs_ref[:, j * W : (j + 1) * W] = rows
        total = total + rows
    score = jnp.sum(total, axis=1, keepdims=True) * (1.0 / 4096.0)
    diag = lax.broadcasted_iota(I32, (Z, W), 0) == lax.broadcasted_iota(I32, (Z, W), 1)
    score_ref[...] = jnp.sum(jnp.where(diag, score, 0.0), axis=0, keepdims=True)[:, :Z]


def exchange(array, axes):
    return lax.all_to_all(array, axes, split_axis=0, concat_axis=0, tiled=True)


def on_device(sliced_state, gate_blocks, gate_slot, samples):
    shape = jax.ShapeDtypeStruct
    state = sliced_state.reshape(Z, 2, X, 32, W)
    packed = pl.pallas_call(pack_kernel, out_shape=shape((Z * X, 40, W), BF), in_specs=[VM, VM], out_specs=VM, name="pack")(
        state, gate_blocks.reshape(2 * W, W)
    )
    packed = exchange(packed, ("z", "x"))
    plane = pl.pallas_call(
        sum_kernel,
        out_shape=shape((X * M, 64, W), BF),
        in_specs=[SM, VM],
        out_specs=VM,
        scratch_shapes=[pltpu.VMEM((32, W), F32)],
        name="sum",
    )(gate_slot, packed)
    plane = exchange(plane, ("x", "y", "k"))
    amplitudes, picked = pl.pallas_call(
        apply_kernel,
        out_shape=(shape((1, 16, 2, W), F32), shape((Z, 40, W), BF)),
        in_specs=[VM, VM],
        out_specs=(VM, VM),
        scratch_shapes=[pltpu.VMEM((X, 2, W, W), F32), pltpu.VMEM((32, W), F32)],
        name="apply",
    )(samples, plane)
    picked = exchange(picked, "z")
    probs, score = pl.pallas_call(
        finish_kernel,
        out_shape=(shape((Z, 4096), F32), shape((1, Z), F32)),
        in_specs=[VM],
        out_specs=(VM, VM),
        scratch_shapes=[pltpu.VMEM((Z * 32, W), F32)],
        name="finish",
    )(picked)
    return amplitudes, probs, score.reshape(Z)


def solution(mesh):
    split = Mesh(mesh.devices.reshape(Z, X, Y, K), ("z", "x", "y", "k"))
    placed = (P(None, ("z", "x"), None, ("y", "k"), None, None), P(("z", "x"), None, None, None), P(), P())
    return jax.shard_map(
        on_device,
        mesh=split,
        in_specs=placed,
        out_specs=(P(("z", "x"), ("y", "k"), None, None), P(), P()),
        check_vma=False,
    )
```

time: 330 us -> 66.7 us (0.20)
  waiting for transfers between devices: 211 us -> 0 us
  starting transfers between devices: 24.1 us -> 0 us
  matrix products: 14 us -> 0 us
  between operations: 14 us -> 0.63 us
  Pallas kernels: 0 us -> 8.96 us
  local copies, waits for them, and re-layouts: 6.8 us -> 0 us
  other arithmetic: 5.13 us -> 0 us
    psum x4 -> x0, waiting for transfers between devices: 163 us -> none  [by_axis(): return functools.reduce(lax.psum, axes, array)]
    all_to_all x0 -> x3, blocking collectives: none -> 56.7 us  [exchange(): return lax.all_to_all(array, axes, split_axis=0, concat_axis=0, tiled=True)]
    psum x4 -> x0, blocking collectives: 42 us -> none  [by_axis(): return functools.reduce(lax.psum, axes, array)]
    all_to_all x3 -> x0, waiting for transfers between devices: 24.5 us -> none  [the longest x1 10.1 us: sum_at_owner(): lax.all_to_all(tiles, axis, split_axis=0, concat_axis=0, tiled=True)]
    all_to_all x3 -> x0, starting transfers between devices: 23.7 us -> none  [the longest x1 9.15 us: on_device(): lax.all_to_all(summed.astype(jnp.bfloat16), MODE, split_axis=2, concat_ax...]
    all_gather x1 -> x0, waiting for transfers between devices: 23.6 us -> none  [gathered_by_axis(): nearer = lax.all_gather(array, axes[-1], axis=dim, tiled=True)]
    dot_general x9 -> x0, matrix products: 14 us -> none  [the longest x4 9.17 us: select_rows(): jnp.dot(onehot, table.reshape(count, -1), preferred_element_type=jnp.floa...]
    all_gather x1 -> x0, blocking collectives: 12.4 us -> none  [gathered_by_axis(): nearer = lax.all_gather(array, axes[-1], axis=dim, tiled=True)]
  transfers between devices with their start and end apart: 8 -> 0, of which waited for: 7 -> 0; matrix products, arithmetic and copies ran while one was open for 1% -> 0% of each run, Pallas kernels for 0% -> 0%
where the time goes in v1:
time: 66.7 us; the launch traced here: 66.3 us
  blocking collectives  56.7 us (85%)
  Pallas kernels  8.96 us (13%)
    all_to_all x3, blocking collectives, exchange(): return lax.all_to_all(array, axes, split_axis=0, concat_axis=0, tiled=True)  56.7 us
    pallas_call x1, Pallas kernels, on_device(): pl.pallas_call(apply_kernel, out_shape=(shape((1, 16, 2, W), F32), shape(...  3.6 us
    pallas_call x1, Pallas kernels, on_device(): pl.pallas_call(sum_kernel, out_shape=shape((X * M, 64, W), BF), in_specs=...  1.88 us
    pallas_call x1, Pallas kernels, on_device(): pl.pallas_call(pack_kernel, out_shape=shape((Z * X, 40, W), BF), in_specs...  1.83 us
    pallas_call x1, Pallas kernels, on_device(): pl.pallas_call(finish_kernel, out_shape=(shape((Z, 4096), F32), shape((1,...  1.65 us

profile of v1, /device:TPU:1, one launch (start us, length us, event | category | flops | bytes accessed | tf_op | source)
XLA Modules:
  0.0 66.3 jit_solution(12979281064042135088)
XLA Ops:
  0.6 1.8 %pack.1 = bf16[32,40,128]{2,1,0:T(8,128)(2,1)} custom-call(bf16[8,2,4,32,128]{4,3,2,1,0:T(8,128)(2,1)} %bitcast.3, bf16[256,128]{1,0:T(8,128)(2,1)} %bitcast.4), custom_call_target="tpu_custom_call" | custom-call | tf_op jit(solution)/shard_map/pack/pallas_call | solution.py:131
  2.5 24.7 %all_to_all.15.in_ref = bf16[32,40,128]{2,1,0:T(8,128)(2,1)} all-to-all(bf16[32,40,128]{2,1,0:T(8,128)(2,1)} %pack.1), channel_id=1, replica_groups=mesh['z'=8,'x'=4,'y'=4,'k'=2] {'z','x'}, dimensions={0} | all-to-all | bytes 655360 | tf_op jit(solution)/shard_map/all_to_all | solution.py:125
  27.1 1.9 %sum.1 = bf16[32,64,128]{2,1,0:T(8,128)(2,1)} custom-call(s32[32]{0:T(128)} %slot_ref.1, bf16[32,40,128]{2,1,0:T(8,128)(2,1)} %all_to_all.15.in_ref), custom_call_target="tpu_custom_call" | custom-call | tf_op jit(solution)/shard_map/sum/pallas_call | solution.py:135
  29.0 19.9 %all_to_all.16.in_ref = bf16[32,64,128]{2,1,0:T(8,128)(2,1)} all-to-all(bf16[32,64,128]{2,1,0:T(8,128)(2,1)} %sum.1), channel_id=1, replica_groups=mesh['z'=8,'x'=4,'y'=4,'k'=2] {'x','y','k'}, dimensions={0} | all-to-all | bytes 1048576 | tf_op jit(solution)/shard_map/all_to_all | solution.py:125
  48.9 3.6 %apply.1 = (f32[1,16,2,128]{3,2,1,0:T(2,128)}, bf16[8,40,128]{2,1,0:T(8,128)(2,1)}) custom-call(s32[8,4096]{1,0:T(8,128)} %samples_ref.1, bf16[32,64,128]{2,1,0:T(8,128)(2,1)} %all_to_all.16.in_ref), custom_call_target="tpu_custom_call" | custom-call | tf_op jit(solution)/shard_map/apply/pallas_call | solution.py:144
  52.5 12.1 %all_to_all.17.in_ref = bf16[8,40,128]{2,1,0:T(8,128)(2,1)} all-to-all(bf16[8,40,128]{2,1,0:T(8,128)(2,1)} %get-tuple-element.8), channel_id=1, replica_groups=mesh['z'=8,'x'=4,'y'=4,'k'=2] {'z'}, dimensions={0} | all-to-all | bytes 163840 | tf_op jit(solution)/shard_map/all_to_all | solution.py:125
  64.6 1.6 %finish.1 = (f32[8,4096]{1,0:T(8,128)}, f32[1,8]{1,0:T(1,128)}) custom-call(bf16[8,40,128]{2,1,0:T(8,128)(2,1)} %all_to_all.17.in_ref), custom_call_target="tpu_custom_call" | custom-call | tf_op jit(solution)/shard_map/finish/pallas_call | solution.py:153

commit v2 on v1

--- a/solution.py
+++ b/solution.py
@@ -12,7 +12,9 @@
 Z, X, Y, K = 8, 4, 4, 2
 M = Y * K
 W = 128
+CP = pltpu.CompilerParams(vmem_limit_bytes=8 * 2**20)
 VM = pl.BlockSpec(memory_space=pltpu.VMEM)
+HB = pl.BlockSpec(memory_space=pltpu.HBM)
 SM = pl.BlockSpec(memory_space=pltpu.SMEM)
 
 
@@ -24,17 +26,21 @@
     return jnp.dot(a, b, preferred_element_type=F32)
 
 
-def pack_kernel(state_ref, gates_ref, out_ref):
-    mode = mode_index()
+def pack_kernel(state_ref, gates_ref, out_ref, held_ref, rows_ref, sems):
+    copies = [pltpu.make_async_copy(state_ref.at[c], held_ref.at[c], sems.at[c]) for c in range(Z)]
+    for copy in copies:
+        copy.start()
+    rows = pltpu.make_async_copy(gates_ref.at[:, mode_index()], rows_ref, sems.at[Z])
+    rows.start()
     for c in range(Z):
+        copies[c].wait()
         for s in range(X):
-            total = state_ref[c, 0, s].astype(F32) + state_ref[c, 1, s].astype(F32)
+            total = held_ref[c, 0, s].astype(F32) + held_ref[c, 1, s].astype(F32)
             out_ref[c * X + s, 0:32, :] = total.astype(BF)
+    rows.wait()
     for s in range(X):
-        start = pl.multiple_of((s * M + mode) * 8, 8)
-        rows = gates_ref[pl.ds(start, 8), :]
         for c in range(Z):
-            out_ref[c * X + s, 32:40, :] = rows
+            out_ref[c * X + s, 32:40, :] = rows_ref[s]
 
 
 def sum_kernel(slot_ref, in_ref, out_ref, sum_ref):
@@ -45,7 +51,7 @@
     sum_ref[...] = total
     state = jnp.concatenate([sum_ref[pl.ds(0, 16, stride=2), :], sum_ref[pl.ds(1, 16, stride=2), :]], axis=0).astype(BF)
     gates = [in_ref[slot_ref[circuit * 4 + b], 32:40, :] for b in range(4)]
-    for i in range(X * M):
+    for i in range(X * Y):
         out_ref[i, 0:32, :] = state
         for b in range(4):
             out_ref[i, 32 + 8 * b : 40 + 8 * b, :] = gates[b]
@@ -60,18 +66,21 @@
     return dot(left, embed(second[:W], second[W:]))
 
 
-def apply_kernel(samples_ref, in_ref, amp_ref, out_ref, full_ref, pick_ref):
+def apply_kernel(samples_ref, own_ref, pair_ref, amp_ref, out_ref, in_ref, full_ref, pick_ref):
     circuit = lax.axis_index("z")
     spect = lax.axis_index("x")
+    core = lax.axis_index("k")
     mode = mode_index()
-    g = [in_ref[:, 32 + 8 * b : 40 + 8 * b, :].reshape(2 * W, W) for b in range(4)]
+    in_ref[:, core] = own_ref[...]
+    in_ref[:, 1 - core] = pair_ref[...]
+    g = [in_ref[:, :, 32 + 8 * b : 40 + 8 * b, :].reshape(2 * W, W) for b in range(4)]
     col = compose(g[0], g[2]).astype(BF)
     row = compose(g[1], g[3])
     row_r, row_i = row[:, :W].T.astype(BF), row[:, W:].T.astype(BF)
     gate_q = embed(col[:, :W], col[:, W:])
     gate_p = jnp.concatenate([jnp.concatenate([row_r, -row_i], axis=1), jnp.concatenate([row_i, row_r], axis=1)], axis=0)
-    real = in_ref[:, 0:16, :].reshape(X * W, W)
-    imag = in_ref[:, 16:32, :].reshape(X * W, W)
+    real = in_ref[:, :, 0:16, :].reshape(X * W, W)
+    imag = in_ref[:, :, 16:32, :].reshape(X * W, W)
     mid = dot(jnp.concatenate([real, imag], axis=1), gate_q).astype(BF)
     mid = jnp.concatenate(
         [jnp.concatenate([mid[s * W : (s + 1) * W, r * W : (r + 1) * W] for s in range(X)], axis=1) for r in range(2)], axis=0
@@ -121,6 +130,10 @@
     score_ref[...] = jnp.sum(jnp.where(diag, score, 0.0), axis=0, keepdims=True)[:, :Z]
 
 
+def hbm(array):
+    return pltpu.with_memory_space_constraint(array, pltpu.HBM)
+
+
 def exchange(array, axes):
     return lax.all_to_all(array, axes, split_axis=0, concat_axis=0, tiled=True)
 
@@ -128,27 +141,29 @@
 def on_device(sliced_state, gate_blocks, gate_slot, samples):
     shape = jax.ShapeDtypeStruct
     state = sliced_state.reshape(Z, 2, X, 32, W)
-    packed = pl.pallas_call(pack_kernel, out_shape=shape((Z * X, 40, W), BF), in_specs=[VM, VM], out_specs=VM, name="pack")(
-        state, gate_blocks.reshape(2 * W, W)
+    packed = pl.pallas_call(pack_kernel, out_shape=shape((Z * X, 40, W), BF), in_specs=[HB, HB], out_specs=VM, compiler_params=CP, name="pack",
+        scratch_shapes=[pltpu.VMEM((Z, 2, X, 32, W), BF), pltpu.VMEM((X, 8, W), BF), pltpu.SemaphoreType.DMA((Z + 1,))])(
+        hbm(state), hbm(gate_blocks.reshape(X, M, 8, W))
     )
     packed = exchange(packed, ("z", "x"))
     plane = pl.pallas_call(
         sum_kernel,
-        out_shape=shape((X * M, 64, W), BF),
+        out_shape=shape((X * Y, 64, W), BF),
         in_specs=[SM, VM],
         out_specs=VM,
         scratch_shapes=[pltpu.VMEM((32, W), F32)],
-        name="sum",
+        compiler_params=CP, name="sum",
     )(gate_slot, packed)
-    plane = exchange(plane, ("x", "y", "k"))
+    plane = exchange(plane, ("x", "y"))
+    pair = lax.ppermute(plane, "k", [(0, 1), (1, 0)])
     amplitudes, picked = pl.pallas_call(
         apply_kernel,
         out_shape=(shape((1, 16, 2, W), F32), shape((Z, 40, W), BF)),
-        in_specs=[VM, VM],
+        in_specs=[VM, VM, VM],
         out_specs=(VM, VM),
-        scratch_shapes=[pltpu.VMEM((X, 2, W, W), F32), pltpu.VMEM((32, W), F32)],
-        name="apply",
-    )(samples, plane)
+        scratch_shapes=[pltpu.VMEM((X * Y, K, 64, W), BF), pltpu.VMEM((X, 2, W, W), F32), pltpu.VMEM((32, W), F32)],
+        compiler_params=CP, name="apply",
+    )(samples, plane, pair)
     picked = exchange(picked, "z")
     probs, score = pl.pallas_call(
         finish_kernel,
@@ -156,7 +171,7 @@
         in_specs=[VM],
         out_specs=(VM, VM),
         scratch_shapes=[pltpu.VMEM((Z * 32, W), F32)],
-        name="finish",
+        compiler_params=CP, name="finish",
     )(picked)
     return amplitudes, probs, score.reshape(Z)
 

time: 66.7 us -> 57.6 us (0.86)
  blocking collectives: 56.7 us -> 47.2 us
  Pallas kernels: 8.96 us -> 4.88 us
  starting transfers between devices: 0 us -> 3.4 us
  waiting for transfers between devices: 0 us -> 1.16 us
    all_to_all x3, blocking collectives: 56.7 us -> 47.2 us  [exchange(): return lax.all_to_all(array, axes, split_axis=0, concat_axis=0, tiled=True)]
    ppermute x0 -> x1, starting transfers between devices: none -> 3.4 us  [on_device(): pair = lax.ppermute(plane, 'k', [(0, 1), (1, 0)])]
    pallas_call x1, Pallas kernels: 1.88 us -> 0.61 us  [on_device(): pl.pallas_call(sum_kernel, out_shape=shape((X * Y, 64, W), BF), in_specs=...]
    pallas_call x1, Pallas kernels: 3.6 us -> 2.36 us  [on_device(): pl.pallas_call(apply_kernel, out_shape=(shape((1, 16, 2, W), F32), shape(...]
    ppermute x0 -> x1, waiting for transfers between devices: none -> 1.16 us  [on_device(): pair = lax.ppermute(plane, 'k', [(0, 1), (1, 0)])]
    pallas_call x1, Pallas kernels: 1.65 us -> 0.76 us  [on_device(): pl.pallas_call(finish_kernel, out_shape=(shape((Z, 4096), F32), shape((1,...]
  transfers between devices with their start and end apart: 0 -> 1, of which waited for: 0 -> 1; matrix products, arithmetic and copies ran while one was open for 0% -> 0% of each run, Pallas kernels for 0% -> 0%
where the time goes in v2:
time: 57.6 us; the launch traced here: 57.3 us
  blocking collectives  47.2 us (82%)
  Pallas kernels  4.88 us (8%)
  starting transfers between devices  3.4 us (6%)
  waiting for transfers between devices  1.16 us (2%)
  between operations  0.67 us (1%)
    all_to_all x3, blocking collectives, exchange(): return lax.all_to_all(array, axes, split_axis=0, concat_axis=0, tiled=True)  47.2 us
    ppermute x1, starting transfers between devices, on_device(): pair = lax.ppermute(plane, 'k', [(0, 1), (1, 0)])  3.4 us
    pallas_call x1, Pallas kernels, on_device(): pl.pallas_call(apply_kernel, out_shape=(shape((1, 16, 2, W), F32), shape(...  2.36 us
    ppermute x1, waiting for transfers between devices, on_device(): pair = lax.ppermute(plane, 'k', [(0, 1), (1, 0)])  1.16 us
    pallas_call x1, Pallas kernels, on_device(): pl.pallas_call(pack_kernel, out_shape=shape((Z * X, 40, W), BF), in_specs...  1.16 us
  transfers between devices with their start and end apart: 1, of which 1 were waited for; matrix products, arithmetic and copies ran while one was open for 0% of the time, Pallas kernels for 0%

profile of v2, /device:TPU:1, one launch (start us, length us, event | category | flops | bytes accessed | tf_op | source)
XLA Modules:
  0.0 57.3 jit_solution(7604493610560336731)
XLA Ops:
  0.6 1.2 %pack.1 = bf16[32,40,128]{2,1,0:T(8,128)(2,1)S(1)} custom-call(bf16[8,2,4,32,128]{4,3,2,1,0:T(8,128)(2,1)} %bitcast.3, bf16[4,8,8,128]{3,2,1,0:T(8,128)(2,1)} %bitcast.4), custom_call_target="tpu_custom_call" | custom-call | tf_op jit(solution)/shard_map/pack/pallas_call | solution.py:144
  1.8 0.0 copy-start.1
  1.8 24.4 %all_to_all.15.in_ref = bf16[32,40,128]{2,1,0:T(8,128)(2,1)S(1)} all-to-all(bf16[32,40,128]{2,1,0:T(8,128)(2,1)S(1)} %pack.1), channel_id=1, replica_groups=mesh['z'=8,'x'=4,'y'=4,'k'=2] {'z','x'}, dimensions={0} | all-to-all | bytes 655360 | tf_op jit(solution)/shard_map/all_to_all | solution.py:138
  26.2 0.0 copy-done.1
  26.2 0.6 %sum.1 = bf16[16,64,128]{2,1,0:T(8,128)(2,1)S(1)} custom-call(s32[32]{0:T(128)S(1)} %copy-done.1, bf16[32,40,128]{2,1,0:T(8,128)(2,1)S(1)} %all_to_all.15.in_ref), custom_call_target="tpu_custom_call" | custom-call | tf_op jit(solution)/shard_map/sum/pallas_call | solution.py:149
  26.8 0.0 copy-start
  26.8 13.2 %all_to_all.16.own_ref = bf16[16,64,128]{2,1,0:T(8,128)(2,1)S(1)} all-to-all(bf16[16,64,128]{2,1,0:T(8,128)(2,1)S(1)} %sum.1), channel_id=1, replica_groups=mesh['z'=8,'x'=4,'y'=4,'k'=2] {'x','y'}, dimensions={0} | all-to-all | bytes 524288 | tf_op jit(solution)/shard_map/all_to_all | solution.py:138
  40.0 3.4 %collective-permute-start = (bf16[16,64,128]{2,1,0:T(8,128)(2,1)S(1)}, bf16[16,64,128]{2,1,0:T(8,128)(2,1)S(1)}, u32[]{:S(2)}, u32[]{:S(2)}) collective-permute-start(bf16[16,64,128]{2,1,0:T(8,128)(2,1)S(1)} %all_to_all.16.own_ref), channel_id=1, source_target_pairs={{0,1},{1,0},{2,3},{3,2},{4,5},{5,4},{6,7},{7,6},{8,9},{9,8},{10,11... | collective-permute-start | bytes 786440 | tf_op jit(solution)/shard_map/ppermute | solution.py:158
  43.4 1.2 %collective-permute-done.pair_ref = bf16[16,64,128]{2,1,0:T(8,128)(2,1)S(1)} collective-permute-done((bf16[16,64,128]{2,1,0:T(8,128)(2,1)S(1)}, bf16[16,64,128]{2,1,0:T(8,128)(2,1)S(1)}, u32[]{:S(2)}, u32[]{:S(2)}) %collective-permute-start) | collective-permute-done | bytes 262176 | tf_op jit(solution)/shard_map/ppermute | solution.py:158
  44.5 0.0 copy-done
  44.5 2.4 %apply.1 = (f32[1,16,2,128]{3,2,1,0:T(2,128)}, bf16[8,40,128]{2,1,0:T(8,128)(2,1)S(1)}) custom-call(s32[8,4096]{1,0:T(8,128)S(1)} %copy-done, bf16[16,64,128]{2,1,0:T(8,128)(2,1)S(1)} %all_to_all.16.own_ref, bf16[16,64,128]{2,1,0:T(8,128)(2,1)S(1)} %collective-permute-done.pair_ref), custom_call_target="tpu_custom_call" | custom-call | tf_op jit(solution)/shard_map/apply/pallas_call | solution.py:159
  46.9 9.7 %all_to_all.17.in_ref = bf16[8,40,128]{2,1,0:T(8,128)(2,1)S(1)} all-to-all(bf16[8,40,128]{2,1,0:T(8,128)(2,1)S(1)} %get-tuple-element.8), channel_id=1, replica_groups=mesh['z'=8,'x'=4,'y'=4,'k'=2] {'z'}, dimensions={0} | all-to-all | bytes 163840 | tf_op jit(solution)/shard_map/all_to_all | solution.py:138
  56.6 0.8 %finish.1 = (f32[8,4096]{1,0:T(8,128)}, f32[1,8]{1,0:T(1,128)}) custom-call(bf16[8,40,128]{2,1,0:T(8,128)(2,1)S(1)} %all_to_all.17.in_ref), custom_call_target="tpu_custom_call" | custom-call | tf_op jit(solution)/shard_map/finish/pallas_call | solution.py:168
Async XLA Ops:
  1.8 24.4 %copy-start.1 = (s32[32]{0:T(128)S(1)}, s32[32]{0:T(128)}, u32[]{:S(2)}) copy-start(s32[32]{0:T(128)} %slot_ref.1) | copy-start | bytes 388
  26.8 17.8 %copy-start = (s32[8,4096]{1,0:T(8,128)S(1)}, s32[8,4096]{1,0:T(8,128)}, u32[]{:S(2)}) copy-start(s32[8,4096]{1,0:T(8,128)} %samples_ref.1) | copy-start | bytes 393220
  40.0 4.6 %collective-permute-start = (bf16[16,64,128]{2,1,0:T(8,128)(2,1)S(1)}, bf16[16,64,128]{2,1,0:T(8,128)(2,1)S(1)}, u32[]{:S(2)}, u32[]{:S(2)}) collective-permute-start(bf16[16,64,128]{2,1,0:T(8,128)(2,1)S(1)} %all_to_all.16.own_ref), channel_id=1, source_target_pairs={{0,1},{1,0},{2,3},{3,2},{4,5},{5,4},{6,7},{7,6},{8,9},{9,8},{10,11... | collective-permute-start | bytes 786440 | tf_op jit(solution)/shard_map/ppermute | solution.py:158

commit v3 on v2

--- a/solution.py
+++ b/solution.py
@@ -12,10 +12,24 @@
 Z, X, Y, K = 8, 4, 4, 2
 M = Y * K
 W = 128
+Z_FIRST, X_FIRST, Y_FIRST = 4, 2, 2
 CP = pltpu.CompilerParams(vmem_limit_bytes=8 * 2**20)
 VM = pl.BlockSpec(memory_space=pltpu.VMEM)
 HB = pl.BlockSpec(memory_space=pltpu.HBM)
 SM = pl.BlockSpec(memory_space=pltpu.SMEM)
+
+
+def led_by(first, count):
+    return [first] + [i for i in range(count) if i != first]
+
+
+Z_ORDER, X_ORDER, Y_ORDER = led_by(Z_FIRST, Z), led_by(X_FIRST, X), led_by(Y_FIRST, Y)
+ZX_ORDER = [z * X + x for z in Z_ORDER for x in X_ORDER]
+XY_ORDER = [x * Y + y for x in X_ORDER for y in Y_ORDER]
+
+
+def place(index, first):
+    return jnp.where(index == first, 0, jnp.where(index < first, index + 1, index))
 
 
 def mode_index():
@@ -36,11 +50,11 @@
         copies[c].wait()
         for s in range(X):
             total = held_ref[c, 0, s].astype(F32) + held_ref[c, 1, s].astype(F32)
-            out_ref[c * X + s, 0:32, :] = total.astype(BF)
+            out_ref[ZX_ORDER.index(c * X + s), 0:32, :] = total.astype(BF)
     rows.wait()
     for s in range(X):
         for c in range(Z):
-            out_ref[c * X + s, 32:40, :] = rows_ref[s]
+            out_ref[ZX_ORDER.index(c * X + s), 32:40, :] = rows_ref[s]
 
 
 def sum_kernel(slot_ref, in_ref, out_ref, sum_ref):
@@ -50,7 +64,8 @@
         total = total + in_ref[i, 0:32, :].astype(F32)
     sum_ref[...] = total
     state = jnp.concatenate([sum_ref[pl.ds(0, 16, stride=2), :], sum_ref[pl.ds(1, 16, stride=2), :]], axis=0).astype(BF)
-    gates = [in_ref[slot_ref[circuit * 4 + b], 32:40, :] for b in range(4)]
+    slots = [slot_ref[circuit * 4 + b] for b in range(4)]
+    gates = [in_ref[place(slot // X, Z_FIRST) * X + place(slot % X, X_FIRST), 32:40, :] for slot in slots]
     for i in range(X * Y):
         out_ref[i, 0:32, :] = state
         for b in range(4):
@@ -71,8 +86,9 @@
     spect = lax.axis_index("x")
     core = lax.axis_index("k")
     mode = mode_index()
-    in_ref[:, core] = own_ref[...]
-    in_ref[:, 1 - core] = pair_ref[...]
+    for i, at in enumerate(XY_ORDER):
+        in_ref[at, core] = own_ref[i]
+        in_ref[at, 1 - core] = pair_ref[i]
     g = [in_ref[:, :, 32 + 8 * b : 40 + 8 * b, :].reshape(2 * W, W) for b in range(4)]
     col = compose(g[0], g[2]).astype(BF)
     row = compose(g[1], g[3])
@@ -115,11 +131,12 @@
         out_ref[c, 32:40, :] = tail
 
 
-def finish_kernel(in_ref, probs_ref, score_ref, wide_ref):
-    for c in range(Z):
-        tail = in_ref[c, 32:40, :].astype(F32)
+def finish_kernel(in_ref, held_ref, probs_ref, score_ref, amp_ref, wide_ref):
+    amp_ref[...] = held_ref[...]
+    for i, c in enumerate(Z_ORDER):
+        tail = in_ref[i, 32:40, :].astype(F32)
         norm = tail[0:1] + tail[1:2]
-        wide_ref[c * 32 : (c + 1) * 32, :] = in_ref[c, 0:32, :].astype(F32) * 65536.0 / norm
+        wide_ref[c * 32 : (c + 1) * 32, :] = in_ref[i, 0:32, :].astype(F32) * 65536.0 / norm
     total = jnp.zeros((Z, W), F32)
     for j in range(32):
         rows = wide_ref[pl.ds(j, Z, stride=32), :]
@@ -134,8 +151,8 @@
     return pltpu.with_memory_space_constraint(array, pltpu.HBM)
 
 
-def exchange(array, axes):
-    return lax.all_to_all(array, axes, split_axis=0, concat_axis=0, tiled=True)
+def exchange(array, axes, order):
+    return lax.all_to_all(array, axes, split_axis=0, concat_axis=0, tiled=True, axis_index_groups=[order])
 
 
 def on_device(sliced_state, gate_blocks, gate_slot, samples):
@@ -145,7 +162,7 @@
         scratch_shapes=[pltpu.VMEM((Z, 2, X, 32, W), BF), pltpu.VMEM((X, 8, W), BF), pltpu.SemaphoreType.DMA((Z + 1,))])(
         hbm(state), hbm(gate_blocks.reshape(X, M, 8, W))
     )
-    packed = exchange(packed, ("z", "x"))
+    packed = exchange(packed, ("z", "x"), ZX_ORDER)
     plane = pl.pallas_call(
         sum_kernel,
         out_shape=shape((X * Y, 64, W), BF),
@@ -154,7 +171,7 @@
         scratch_shapes=[pltpu.VMEM((32, W), F32)],
         compiler_params=CP, name="sum",
     )(gate_slot, packed)
-    plane = exchange(plane, ("x", "y"))
+    plane = exchange(plane, ("x", "y"), XY_ORDER)
     pair = lax.ppermute(plane, "k", [(0, 1), (1, 0)])
     amplitudes, picked = pl.pallas_call(
         apply_kernel,
@@ -164,15 +181,15 @@
         scratch_shapes=[pltpu.VMEM((X * Y, K, 64, W), BF), pltpu.VMEM((X, 2, W, W), F32), pltpu.VMEM((32, W), F32)],
         compiler_params=CP, name="apply",
     )(samples, plane, pair)
-    picked = exchange(picked, "z")
-    probs, score = pl.pallas_call(
+    picked = exchange(picked, "z", Z_ORDER)
+    probs, score, amplitudes = pl.pallas_call(
         finish_kernel,
-        out_shape=(shape((Z, 4096), F32), shape((1, Z), F32)),
-        in_specs=[VM],
-        out_specs=(VM, VM),
+        out_shape=(shape((Z, 4096), F32), shape((1, Z), F32), shape((1, 16, 2, W), F32)),
+        in_specs=[VM, VM],
+        out_specs=(VM, VM, VM),
         scratch_shapes=[pltpu.VMEM((Z * 32, W), F32)],
         compiler_params=CP, name="finish",
-    )(picked)
+    )(picked, amplitudes)
     return amplitudes, probs, score.reshape(Z)
 
 

time: 57.6 us -> 50.4 us (0.88)
  blocking collectives: 47.2 us -> 40.8 us
    all_to_all x3, blocking collectives: 47.2 us -> 40.8 us  [exchange(): lax.all_to_all(array, axes, split_axis=0, concat_axis=0, tiled=True, axis...]
where the time goes in v3:
time: 50.4 us; the launch traced here: 50 us
  blocking collectives  40.8 us (81%)
  Pallas kernels  4.42 us (9%)
  starting transfers between devices  3 us (6%)
  waiting for transfers between devices  1.16 us (2%)
  between operations  0.67 us (1%)
    all_to_all x3, blocking collectives, exchange(): lax.all_to_all(array, axes, split_axis=0, concat_axis=0, tiled=True, axis...  40.8 us
    ppermute x1, starting transfers between devices, on_device(): pair = lax.ppermute(plane, 'k', [(0, 1), (1, 0)])  3 us
    pallas_call x1, Pallas kernels, on_device(): pl.pallas_call(apply_kernel, out_shape=(shape((1, 16, 2, W), F32), shape(...  1.86 us
    ppermute x1, waiting for transfers between devices, on_device(): pair = lax.ppermute(plane, 'k', [(0, 1), (1, 0)])  1.16 us
    pallas_call x1, Pallas kernels, on_device(): pl.pallas_call(pack_kernel, out_shape=shape((Z * X, 40, W), BF), in_specs...  1.16 us
  transfers between devices with their start and end apart: 1, of which 1 were waited for; matrix products, arithmetic and copies ran while one was open for 0% of the time, Pallas kernels for 0%

profile of v3, /device:TPU:1, one launch (start us, length us, event | category | flops | bytes accessed | tf_op | source)
XLA Modules:
  0.0 50.0 jit_solution(10259694083371688802)
XLA Ops:
  0.6 1.2 %pack.1 = bf16[32,40,128]{2,1,0:T(8,128)(2,1)S(1)} custom-call(bf16[8,2,4,32,128]{4,3,2,1,0:T(8,128)(2,1)} %bitcast.3, bf16[4,8,8,128]{3,2,1,0:T(8,128)(2,1)} %bitcast.4), custom_call_target="tpu_custom_call" | custom-call | tf_op jit(solution)/shard_map/pack/pallas_call | solution.py:161
  1.8 0.0 copy-start.1
  1.8 21.5 %all_to_all.15.in_ref = bf16[32,40,128]{2,1,0:T(8,128)(2,1)S(1)} all-to-all(bf16[32,40,128]{2,1,0:T(8,128)(2,1)S(1)} %pack.1), channel_id=1, replica_groups={{144,128,136,152,16,0,8,24,48,32,40,56,80,64,72,88,112,96,104,120,176,1..., dimensions={0} | all-to-all | bytes 655360 | tf_op jit(solution)/shard_map/all_to_all | solution.py:155
  23.3 0.0 copy-done.1
  23.3 0.6 %sum.1 = bf16[16,64,128]{2,1,0:T(8,128)(2,1)S(1)} custom-call(s32[32]{0:T(128)S(1)} %copy-done.1, bf16[32,40,128]{2,1,0:T(8,128)(2,1)S(1)} %all_to_all.15.in_ref), custom_call_target="tpu_custom_call" | custom-call | tf_op jit(solution)/shard_map/sum/pallas_call | solution.py:166
  23.9 0.0 copy-start
  23.9 10.4 %all_to_all.16.own_ref = bf16[16,64,128]{2,1,0:T(8,128)(2,1)S(1)} all-to-all(bf16[16,64,128]{2,1,0:T(8,128)(2,1)S(1)} %sum.1), channel_id=1, replica_groups={{20,16,18,22,4,0,2,6,12,8,10,14,28,24,26,30},{21,17,19,23,5,1,3,7,13,9,..., dimensions={0} | all-to-all | bytes 524288 | tf_op jit(solution)/shard_map/all_to_all | solution.py:155
  34.4 3.0 %collective-permute-start = (bf16[16,64,128]{2,1,0:T(8,128)(2,1)S(1)}, bf16[16,64,128]{2,1,0:T(8,128)(2,1)S(1)}, u32[]{:S(2)}, u32[]{:S(2)}) collective-permute-start(bf16[16,64,128]{2,1,0:T(8,128)(2,1)S(1)} %all_to_all.16.own_ref), channel_id=1, source_target_pairs={{0,1},{1,0},{2,3},{3,2},{4,5},{5,4},{6,7},{7,6},{8,9},{9,8},{10,11... | collective-permute-start | bytes 786440 | tf_op jit(solution)/shard_map/ppermute | solution.py:175
  37.4 1.2 %collective-permute-done.pair_ref = bf16[16,64,128]{2,1,0:T(8,128)(2,1)S(1)} collective-permute-done((bf16[16,64,128]{2,1,0:T(8,128)(2,1)S(1)}, bf16[16,64,128]{2,1,0:T(8,128)(2,1)S(1)}, u32[]{:S(2)}, u32[]{:S(2)}) %collective-permute-start) | collective-permute-done | bytes 262176 | tf_op jit(solution)/shard_map/ppermute | solution.py:175
  38.5 0.0 copy-done
  38.5 1.9 %apply.1 = (f32[1,16,2,128]{3,2,1,0:T(2,128)S(1)}, bf16[8,40,128]{2,1,0:T(8,128)(2,1)S(1)}) custom-call(s32[8,4096]{1,0:T(8,128)S(1)} %copy-done, bf16[16,64,128]{2,1,0:T(8,128)(2,1)S(1)} %all_to_all.16.own_ref, bf16[16,64,128]{2,1,0:T(8,128)(2,1)S(1)} %collective-permute-done.pair_ref), custom_call_target="tpu_custom_call" | custom-call | tf_op jit(solution)/shard_map/apply/pallas_call | solution.py:176
  40.4 8.8 %all_to_all.17.in_ref = bf16[8,40,128]{2,1,0:T(8,128)(2,1)S(1)} all-to-all(bf16[8,40,128]{2,1,0:T(8,128)(2,1)S(1)} %get-tuple-element.8), channel_id=1, replica_groups={{128,0,32,64,96,160,192,224},{129,1,33,65,97,161,193,225},{130,2,34,66,..., dimensions={0} | all-to-all | bytes 163840 | tf_op jit(solution)/shard_map/all_to_all | solution.py:155
  49.2 0.8 %finish.1 = (f32[8,4096]{1,0:T(8,128)}, f32[1,8]{1,0:T(1,128)}, f32[1,16,2,128]{3,2,1,0:T(2,128)}) custom-call(bf16[8,40,128]{2,1,0:T(8,128)(2,1)S(1)} %all_to_all.17.in_ref, f32[1,16,2,128]{3,2,1,0:T(2,128)S(1)} %get-tuple-element.9.held_ref), custom_call_target="tpu_custom_call" | custom-call | tf_op jit(solution)/shard_map/finish/pallas_call | solution.py:185
Async XLA Ops:
  1.8 21.5 %copy-start.1 = (s32[32]{0:T(128)S(1)}, s32[32]{0:T(128)}, u32[]{:S(2)}) copy-start(s32[32]{0:T(128)} %slot_ref.1) | copy-start | bytes 388
  23.9 14.6 %copy-start = (s32[8,4096]{1,0:T(8,128)S(1)}, s32[8,4096]{1,0:T(8,128)}, u32[]{:S(2)}) copy-start(s32[8,4096]{1,0:T(8,128)} %samples_ref.1) | copy-start | bytes 393220
  34.4 4.2 %collective-permute-start = (bf16[16,64,128]{2,1,0:T(8,128)(2,1)S(1)}, bf16[16,64,128]{2,1,0:T(8,128)(2,1)S(1)}, u32[]{:S(2)}, u32[]{:S(2)}) collective-permute-start(bf16[16,64,128]{2,1,0:T(8,128)(2,1)S(1)} %all_to_all.16.own_ref), channel_id=1, source_target_pairs={{0,1},{1,0},{2,3},{3,2},{4,5},{5,4},{6,7},{7,6},{8,9},{9,8},{10,11... | collective-permute-start | bytes 786440 | tf_op jit(solution)/shard_map/ppermute | solution.py:175

commit v4 on v3

--- a/solution.py
+++ b/solution.py
@@ -15,8 +15,8 @@
 Z_FIRST, X_FIRST, Y_FIRST = 4, 2, 2
 CP = pltpu.CompilerParams(vmem_limit_bytes=8 * 2**20)
 VM = pl.BlockSpec(memory_space=pltpu.VMEM)
+ANY = pl.BlockSpec(memory_space=pl.ANY)
 HB = pl.BlockSpec(memory_space=pltpu.HBM)
-SM = pl.BlockSpec(memory_space=pltpu.SMEM)
 
 
 def led_by(first, count):
@@ -25,11 +25,7 @@
 
 Z_ORDER, X_ORDER, Y_ORDER = led_by(Z_FIRST, Z), led_by(X_FIRST, X), led_by(Y_FIRST, Y)
 ZX_ORDER = [z * X + x for z in Z_ORDER for x in X_ORDER]
-XY_ORDER = [x * Y + y for x in X_ORDER for y in Y_ORDER]
-
-
-def place(index, first):
-    return jnp.where(index == first, 0, jnp.where(index < first, index + 1, index))
+XY_ORDER = [x * Y + y for y in Y_ORDER for x in X_ORDER]
 
 
 def mode_index():
@@ -40,36 +36,43 @@
     return jnp.dot(a, b, preferred_element_type=F32)
 
 
-def pack_kernel(state_ref, gates_ref, out_ref, held_ref, rows_ref, sems):
+def pack_kernel(state_ref, gates_ref, slot_ref, out_ref, slot_out_ref, held_ref, rows_ref, sems):
     copies = [pltpu.make_async_copy(state_ref.at[c], held_ref.at[c], sems.at[c]) for c in range(Z)]
     for copy in copies:
         copy.start()
     rows = pltpu.make_async_copy(gates_ref.at[:, mode_index()], rows_ref, sems.at[Z])
     rows.start()
+    slots = pltpu.make_async_copy(slot_ref, slot_out_ref, sems.at[Z + 1])
+    slots.start()
     for c in range(Z):
         copies[c].wait()
         for s in range(X):
             total = held_ref[c, 0, s].astype(F32) + held_ref[c, 1, s].astype(F32)
             out_ref[ZX_ORDER.index(c * X + s), 0:32, :] = total.astype(BF)
     rows.wait()
+    slots.wait()
     for s in range(X):
         for c in range(Z):
             out_ref[ZX_ORDER.index(c * X + s), 32:40, :] = rows_ref[s]
 
 
 def sum_kernel(slot_ref, in_ref, out_ref, sum_ref):
-    circuit = lax.axis_index("z")
-    total = in_ref[0, 0:32, :].astype(F32)
-    for i in range(1, Z * X):
+    first = lax.axis_index("z") * 4
+    slots = jnp.broadcast_to(slot_ref[...], (8, Z * X))
+    blocks = lax.broadcasted_iota(I32, (8, Z * X), 1) - first
+    wanted = [jnp.sum(jnp.where(blocks == b, slots, 0), axis=1, keepdims=True) for b in range(4)]
+    total = jnp.zeros((32, W), F32)
+    gates = [jnp.zeros((8, W), F32) for _ in range(4)]
+    for i, owner in enumerate(ZX_ORDER):
         total = total + in_ref[i, 0:32, :].astype(F32)
+        rows = in_ref[i, 32:40, :].astype(F32)
+        gates = [jnp.where(wanted[b] == owner, rows, gates[b]) for b in range(4)]
     sum_ref[...] = total
     state = jnp.concatenate([sum_ref[pl.ds(0, 16, stride=2), :], sum_ref[pl.ds(1, 16, stride=2), :]], axis=0).astype(BF)
-    slots = [slot_ref[circuit * 4 + b] for b in range(4)]
-    gates = [in_ref[place(slot // X, Z_FIRST) * X + place(slot % X, X_FIRST), 32:40, :] for slot in slots]
     for i in range(X * Y):
         out_ref[i, 0:32, :] = state
         for b in range(4):
-            out_ref[i, 32 + 8 * b : 40 + 8 * b, :] = gates[b]
+            out_ref[i, 32 + 8 * b : 40 + 8 * b, :] = gates[b].astype(BF)
 
 
 def embed(real, imag):
@@ -81,7 +84,17 @@
     return dot(left, embed(second[:W], second[W:]))
 
 
-def apply_kernel(samples_ref, own_ref, pair_ref, amp_ref, out_ref, in_ref, full_ref, pick_ref):
+def hot_kernel(samples_ref, after_ref, out_ref):
+    flat = samples_ref[pl.ds(lax.axis_index("z"), 1), :]
+    lane = (((flat >> 14) & 1) * W + (flat & 127)).astype(F32).astype(BF)
+    chunk = 512
+    ids = lax.broadcasted_iota(I32, (2 * W, chunk), 0).astype(F32).astype(BF)
+    for j in range(4096 // chunk):
+        hit = ids == lane[:, j * chunk : (j + 1) * chunk]
+        out_ref[:, j * chunk : (j + 1) * chunk] = jnp.where(hit, jnp.ones((), BF), jnp.zeros((), BF))
+
+
+def apply_kernel(samples_ref, hot_ref, own_ref, pair_ref, amp_ref, out_ref, in_ref, full_ref, pick_ref):
     circuit = lax.axis_index("z")
     spect = lax.axis_index("x")
     core = lax.axis_index("k")
@@ -114,11 +127,9 @@
     chunk = 512
     for j in range(4096 // chunk):
         flat = samples_ref[pl.ds(circuit, 1), j * chunk : (j + 1) * chunk]
-        lane = ((flat >> 14) & 1) * W + (flat & 127)
         line = ((flat >> 15) & 1) * W + ((flat >> 7) & 127)
         ids = lax.broadcasted_iota(I32, (2 * W, chunk), 0)
-        onehot = jnp.where(ids == lane, 1.0, 0.0).astype(BF)
-        got = dot(table, onehot)
+        got = dot(table, hot_ref[:, j * chunk : (j + 1) * chunk])
         got = jnp.sum(jnp.where(ids == line, got, 0.0), axis=0, keepdims=True)
         for i in range(chunk // W):
             pick_ref[j * (chunk // W) + i : j * (chunk // W) + i + 1, :] = got[:, i * W : (i + 1) * W]
@@ -158,29 +169,43 @@
 def on_device(sliced_state, gate_blocks, gate_slot, samples):
     shape = jax.ShapeDtypeStruct
     state = sliced_state.reshape(Z, 2, X, 32, W)
-    packed = pl.pallas_call(pack_kernel, out_shape=shape((Z * X, 40, W), BF), in_specs=[HB, HB], out_specs=VM, compiler_params=CP, name="pack",
-        scratch_shapes=[pltpu.VMEM((Z, 2, X, 32, W), BF), pltpu.VMEM((X, 8, W), BF), pltpu.SemaphoreType.DMA((Z + 1,))])(
-        hbm(state), hbm(gate_blocks.reshape(X, M, 8, W))
-    )
+    packed, slots = pl.pallas_call(
+        pack_kernel,
+        out_shape=(shape((Z * X, 40, W), BF), shape((1, Z * X), I32)),
+        in_specs=[HB, HB, HB],
+        out_specs=(VM, VM),
+        scratch_shapes=[pltpu.VMEM((Z, 2, X, 32, W), BF), pltpu.VMEM((X, 8, W), BF), pltpu.SemaphoreType.DMA((Z + 2,))],
+        compiler_params=CP,
+        name="pack",
+    )(hbm(state), hbm(gate_blocks.reshape(X, M, 8, W)), hbm(gate_slot.reshape(1, Z * X)))
     packed = exchange(packed, ("z", "x"), ZX_ORDER)
     plane = pl.pallas_call(
         sum_kernel,
         out_shape=shape((X * Y, 64, W), BF),
-        in_specs=[SM, VM],
+        in_specs=[VM, VM],
         out_specs=VM,
         scratch_shapes=[pltpu.VMEM((32, W), F32)],
         compiler_params=CP, name="sum",
-    )(gate_slot, packed)
+    )(slots, packed)
     plane = exchange(plane, ("x", "y"), XY_ORDER)
     pair = lax.ppermute(plane, "k", [(0, 1), (1, 0)])
+    hot = pl.pallas_call(
+        hot_kernel,
+        out_shape=shape((2 * W, 4096), BF),
+        in_specs=[VM, ANY],
+        out_specs=VM,
+        compiler_params=CP,
+        cost_estimate=pl.CostEstimate(flops=2**22, bytes_accessed=2**21, transcendentals=0),
+        name="hot",
+    )(samples, plane)
     amplitudes, picked = pl.pallas_call(
         apply_kernel,
         out_shape=(shape((1, 16, 2, W), F32), shape((Z, 40, W), BF)),
-        in_specs=[VM, VM, VM],
+        in_specs=[VM, VM, VM, VM],
         out_specs=(VM, VM),
         scratch_shapes=[pltpu.VMEM((X * Y, K, 64, W), BF), pltpu.VMEM((X, 2, W, W), F32), pltpu.VMEM((32, W), F32)],
         compiler_params=CP, name="apply",
-    )(samples, plane, pair)
+    )(samples, hot, plane, pair)
     picked = exchange(picked, "z", Z_ORDER)
     probs, score, amplitudes = pl.pallas_call(
         finish_kernel,

time: 50.4 us -> 49.3 us (0.978)
  Pallas kernels: 4.42 us -> 3.83 us
    pallas_call x1 -> x2, Pallas kernels: 1.16 us -> 1.45 us  [the longest x1 1.2 us: on_device(): pl.pallas_call(pack_kernel, out_shape=(shape((Z * X, 40, W), BF), shape((...]
  transfers between devices with their start and end apart: 1 -> 1, of which waited for: 1 -> 1; matrix products, arithmetic and copies ran while one was open for 0% -> 0% of each run, Pallas kernels for 0% -> 1%
where the time goes in v4:
time: 49.3 us; the launch traced here: 48.7 us
  blocking collectives  40.5 us (82%)
  Pallas kernels  3.83 us (8%)
  starting transfers between devices  2.79 us (6%)
  waiting for transfers between devices  0.91 us (2%)
  between operations  0.66 us (1%)
    all_to_all x3, blocking collectives, exchange(): lax.all_to_all(array, axes, split_axis=0, concat_axis=0, tiled=True, axis...  40.5 us
    ppermute x1, starting transfers between devices, on_device(): pair = lax.ppermute(plane, 'k', [(0, 1), (1, 0)])  2.79 us
    pallas_call x1, Pallas kernels, on_device(): pl.pallas_call(apply_kernel, out_shape=(shape((1, 16, 2, W), F32), shape(...  1.45 us
    pallas_call x1, Pallas kernels, on_device(): pl.pallas_call(pack_kernel, out_shape=(shape((Z * X, 40, W), BF), shape((...  1.2 us
  transfers between devices with their start and end apart: 1, of which 1 were waited for; matrix products, arithmetic and copies ran while one was open for 0% of the time, Pallas kernels for 1%

profile of v4, /device:TPU:1, one launch (start us, length us, event | category | flops | bytes accessed | tf_op | source)
XLA Modules:
  0.0 48.7 jit_solution(339395865992202781)
XLA Ops:
  0.6 0.0 copy-start
  0.6 1.2 %pack.1 = (bf16[32,40,128]{2,1,0:T(8,128)(2,1)S(1)}, s32[1,32]{1,0:T(1,128)S(1)}) custom-call(bf16[8,2,4,32,128]{4,3,2,1,0:T(8,128)(2,1)} %bitcast.4, bf16[4,8,8,128]{3,2,1,0:T(8,128)(2,1)} %bitcast.5, s32[1,32]{1,0:T(1,128)} %bitcast.6), custom_call_target="tpu_custom_call" | custom-call | tf_op jit(solution)/shard_map/pack/pallas_call | solution.py:172
  1.9 21.5 %all_to_all.15.in_ref = bf16[32,40,128]{2,1,0:T(8,128)(2,1)S(1)} all-to-all(bf16[32,40,128]{2,1,0:T(8,128)(2,1)S(1)} %get-tuple-element.11), channel_id=1, replica_groups={{144,128,136,152,16,0,8,24,48,32,40,56,80,64,72,88,112,96,104,120,176,1..., dimensions={0} | all-to-all | bytes 655360 | tf_op jit(solution)/shard_map/all_to_all | solution.py:166
  23.3 0.1 sum.1
  23.5 10.2 %all_to_all.16.after_ref.own_ref = bf16[16,64,128]{2,1,0:T(8,128)(2,1)S(1)} all-to-all(bf16[16,64,128]{2,1,0:T(8,128)(2,1)S(1)} %sum.1), channel_id=1, replica_groups={{20,4,12,28,16,0,8,24,18,2,10,26,22,6,14,30},{21,5,13,29,17,1,9,25,19,3..., dimensions={0} | all-to-all | bytes 524288 | tf_op jit(solution)/shard_map/all_to_all | solution.py:166
  33.7 2.8 %collective-permute-start = (bf16[16,64,128]{2,1,0:T(8,128)(2,1)S(1)}, bf16[16,64,128]{2,1,0:T(8,128)(2,1)S(1)}, u32[]{:S(2)}, u32[]{:S(2)}) collective-permute-start(bf16[16,64,128]{2,1,0:T(8,128)(2,1)S(1)} %all_to_all.16.after_ref.own_ref), channel_id=1, source_target_pairs={{0,1},{1,0},{2,3},{3,2},{4,5},{5,4},{6,7},{7,6},{8,9},{9,8},{10,11... | collective-permute-start | bytes 786440 | tf_op jit(solution)/shard_map/ppermute | solution.py:191
  36.5 0.0 copy-done
  36.5 0.2 hot.1.hot_ref
  36.7 0.9 %collective-permute-done.pair_ref = bf16[16,64,128]{2,1,0:T(8,128)(2,1)S(1)} collective-permute-done((bf16[16,64,128]{2,1,0:T(8,128)(2,1)S(1)}, bf16[16,64,128]{2,1,0:T(8,128)(2,1)S(1)}, u32[]{:S(2)}, u32[]{:S(2)}) %collective-permute-start) | collective-permute-done | bytes 262176 | tf_op jit(solution)/shard_map/ppermute | solution.py:191
  37.6 1.5 %apply.1 = (f32[1,16,2,128]{3,2,1,0:T(2,128)S(1)}, bf16[8,40,128]{2,1,0:T(8,128)(2,1)S(1)}) custom-call(s32[8,4096]{1,0:T(8,128)S(1)} %copy-done, bf16[256,4096]{1,0:T(8,128)(2,1)S(1)} %hot.1.hot_ref, bf16[16,64,128]{2,1,0:T(8,128)(2,1)S(1)} %all_to_all.16.after_ref.own_ref, bf16[16,64,128]{2,1,0:T(8,128)(2,1)S(1)} %collective-permute-done.pair_ref), custom_call_target="tpu_custom_call" | custom-call | tf_op jit(solution)/shard_map/apply/pallas_call | solution.py:201
  39.1 8.8 %all_to_all.17.in_ref = bf16[8,40,128]{2,1,0:T(8,128)(2,1)S(1)} all-to-all(bf16[8,40,128]{2,1,0:T(8,128)(2,1)S(1)} %get-tuple-element.12), channel_id=1, replica_groups={{128,0,32,64,96,160,192,224},{129,1,33,65,97,161,193,225},{130,2,34,66,..., dimensions={0} | all-to-all | bytes 163840 | tf_op jit(solution)/shard_map/all_to_all | solution.py:166
  47.9 0.8 %finish.1 = (f32[8,4096]{1,0:T(8,128)}, f32[1,8]{1,0:T(1,128)}, f32[1,16,2,128]{3,2,1,0:T(2,128)}) custom-call(bf16[8,40,128]{2,1,0:T(8,128)(2,1)S(1)} %all_to_all.17.in_ref, f32[1,16,2,128]{3,2,1,0:T(2,128)S(1)} %get-tuple-element.13.held_ref), custom_call_target="tpu_custom_call" | custom-call | tf_op jit(solution)/shard_map/finish/pallas_call | solution.py:210
Async XLA Ops:
  0.6 35.8 %copy-start = (s32[8,4096]{1,0:T(8,128)S(1)}, s32[8,4096]{1,0:T(8,128)}, u32[]{:S(2)}) copy-start(s32[8,4096]{1,0:T(8,128)} %samples_ref.3) | copy-start | bytes 393220
  33.7 4.0 %collective-permute-start = (bf16[16,64,128]{2,1,0:T(8,128)(2,1)S(1)}, bf16[16,64,128]{2,1,0:T(8,128)(2,1)S(1)}, u32[]{:S(2)}, u32[]{:S(2)}) collective-permute-start(bf16[16,64,128]{2,1,0:T(8,128)(2,1)S(1)} %all_to_all.16.after_ref.own_ref), channel_id=1, source_target_pairs={{0,1},{1,0},{2,3},{3,2},{4,5},{5,4},{6,7},{7,6},{8,9},{9,8},{10,11... | collective-permute-start | bytes 786440 | tf_op jit(solution)/shard_map/ppermute | solution.py:191

commit v5 on v4

--- a/solution.py
+++ b/solution.py
@@ -125,12 +125,16 @@
     norm = jnp.sum(mag)
     table = jnp.concatenate([mag[:, : 2 * W], mag[:, 2 * W :]], axis=0).astype(BF)
     chunk = 512
+    ids = lax.broadcasted_iota(I32, (2 * W, chunk), 0).astype(F32).astype(BF)
     for j in range(4096 // chunk):
         flat = samples_ref[pl.ds(circuit, 1), j * chunk : (j + 1) * chunk]
-        line = ((flat >> 15) & 1) * W + ((flat >> 7) & 127)
-        ids = lax.broadcasted_iota(I32, (2 * W, chunk), 0)
-        got = dot(table, hot_ref[:, j * chunk : (j + 1) * chunk])
-        got = jnp.sum(jnp.where(ids == line, got, 0.0), axis=0, keepdims=True)
+        line = (((flat >> 15) & 1) * W + ((flat >> 7) & 127)).astype(F32).astype(BF)
+        got = dot(table, hot_ref[:, j * chunk : (j + 1) * chunk]).astype(BF)
+        got = jnp.where(ids == line, got, jnp.zeros((), BF))
+        held = got[0:16]
+        for i in range(1, 16):
+            held = held + got[16 * i : 16 * i + 16]
+        got = jnp.sum(held.astype(F32), axis=0, keepdims=True)
         for i in range(chunk // W):
             pick_ref[j * (chunk // W) + i : j * (chunk // W) + i + 1, :] = got[:, i * W : (i + 1) * W]
     picked = pick_ref[...].astype(BF)

time: 49.3 us -> 49.2 us (level)
  no operation moved by 1% of the time
where the time goes in v5:
time: 49.2 us; the launch traced here: 48.6 us
  blocking collectives  40.5 us (82%)
  Pallas kernels  3.73 us (8%)
  starting transfers between devices  2.79 us (6%)
  waiting for transfers between devices  0.91 us (2%)
  between operations  0.66 us (1%)
    all_to_all x3, blocking collectives, exchange(): lax.all_to_all(array, axes, split_axis=0, concat_axis=0, tiled=True, axis...  40.5 us
    ppermute x1, starting transfers between devices, on_device(): pair = lax.ppermute(plane, 'k', [(0, 1), (1, 0)])  2.79 us
    pallas_call x1, Pallas kernels, on_device(): pl.pallas_call(apply_kernel, out_shape=(shape((1, 16, 2, W), F32), shape(...  1.35 us
    pallas_call x1, Pallas kernels, on_device(): pl.pallas_call(pack_kernel, out_shape=(shape((Z * X, 40, W), BF), shape((...  1.2 us
  transfers between devices with their start and end apart: 1, of which 1 were waited for; matrix products, arithmetic and copies ran while one was open for 0% of the time, Pallas kernels for 1%

profile of v5, /device:TPU:1, one launch (start us, length us, event | category | flops | bytes accessed | tf_op | source)
XLA Modules:
  0.0 48.6 jit_solution(12005507874709918804)
XLA Ops:
  0.6 0.0 copy-start
  0.6 1.2 %pack.1 = (bf16[32,40,128]{2,1,0:T(8,128)(2,1)S(1)}, s32[1,32]{1,0:T(1,128)S(1)}) custom-call(bf16[8,2,4,32,128]{4,3,2,1,0:T(8,128)(2,1)} %bitcast.4, bf16[4,8,8,128]{3,2,1,0:T(8,128)(2,1)} %bitcast.5, s32[1,32]{1,0:T(1,128)} %bitcast.6), custom_call_target="tpu_custom_call" | custom-call | tf_op jit(solution)/shard_map/pack/pallas_call | solution.py:176
  1.9 21.5 %all_to_all.15.in_ref = bf16[32,40,128]{2,1,0:T(8,128)(2,1)S(1)} all-to-all(bf16[32,40,128]{2,1,0:T(8,128)(2,1)S(1)} %get-tuple-element.11), channel_id=1, replica_groups={{144,128,136,152,16,0,8,24,48,32,40,56,80,64,72,88,112,96,104,120,176,1..., dimensions={0} | all-to-all | bytes 655360 | tf_op jit(solution)/shard_map/all_to_all | solution.py:170
  23.3 0.1 sum.1
  23.5 10.2 %all_to_all.16.after_ref.own_ref = bf16[16,64,128]{2,1,0:T(8,128)(2,1)S(1)} all-to-all(bf16[16,64,128]{2,1,0:T(8,128)(2,1)S(1)} %sum.1), channel_id=1, replica_groups={{20,4,12,28,16,0,8,24,18,2,10,26,22,6,14,30},{21,5,13,29,17,1,9,25,19,3..., dimensions={0} | all-to-all | bytes 524288 | tf_op jit(solution)/shard_map/all_to_all | solution.py:170
  33.7 2.8 %collective-permute-start = (bf16[16,64,128]{2,1,0:T(8,128)(2,1)S(1)}, bf16[16,64,128]{2,1,0:T(8,128)(2,1)S(1)}, u32[]{:S(2)}, u32[]{:S(2)}) collective-permute-start(bf16[16,64,128]{2,1,0:T(8,128)(2,1)S(1)} %all_to_all.16.after_ref.own_ref), channel_id=1, source_target_pairs={{0,1},{1,0},{2,3},{3,2},{4,5},{5,4},{6,7},{7,6},{8,9},{9,8},{10,11... | collective-permute-start | bytes 786440 | tf_op jit(solution)/shard_map/ppermute | solution.py:195
  36.5 0.0 copy-done
  36.5 0.2 hot.1.hot_ref
  36.7 0.9 %collective-permute-done.pair_ref = bf16[16,64,128]{2,1,0:T(8,128)(2,1)S(1)} collective-permute-done((bf16[16,64,128]{2,1,0:T(8,128)(2,1)S(1)}, bf16[16,64,128]{2,1,0:T(8,128)(2,1)S(1)}, u32[]{:S(2)}, u32[]{:S(2)}) %collective-permute-start) | collective-permute-done | bytes 262176 | tf_op jit(solution)/shard_map/ppermute | solution.py:195
  37.6 1.4 %apply.1 = (f32[1,16,2,128]{3,2,1,0:T(2,128)S(1)}, bf16[8,40,128]{2,1,0:T(8,128)(2,1)S(1)}) custom-call(s32[8,4096]{1,0:T(8,128)S(1)} %copy-done, bf16[256,4096]{1,0:T(8,128)(2,1)S(1)} %hot.1.hot_ref, bf16[16,64,128]{2,1,0:T(8,128)(2,1)S(1)} %all_to_all.16.after_ref.own_ref, bf16[16,64,128]{2,1,0:T(8,128)(2,1)S(1)} %collective-permute-done.pair_ref), custom_call_target="tpu_custom_call" | custom-call | tf_op jit(solution)/shard_map/apply/pallas_call | solution.py:205
  39.0 8.8 %all_to_all.17.in_ref = bf16[8,40,128]{2,1,0:T(8,128)(2,1)S(1)} all-to-all(bf16[8,40,128]{2,1,0:T(8,128)(2,1)S(1)} %get-tuple-element.12), channel_id=1, replica_groups={{128,0,32,64,96,160,192,224},{129,1,33,65,97,161,193,225},{130,2,34,66,..., dimensions={0} | all-to-all | bytes 163840 | tf_op jit(solution)/shard_map/all_to_all | solution.py:170
  47.8 0.8 %finish.1 = (f32[8,4096]{1,0:T(8,128)}, f32[1,8]{1,0:T(1,128)}, f32[1,16,2,128]{3,2,1,0:T(2,128)}) custom-call(bf16[8,40,128]{2,1,0:T(8,128)(2,1)S(1)} %all_to_all.17.in_ref, f32[1,16,2,128]{3,2,1,0:T(2,128)S(1)} %get-tuple-element.13.held_ref), custom_call_target="tpu_custom_call" | custom-call | tf_op jit(solution)/shard_map/finish/pallas_call | solution.py:214
Async XLA Ops:
  0.6 35.8 %copy-start = (s32[8,4096]{1,0:T(8,128)S(1)}, s32[8,4096]{1,0:T(8,128)}, u32[]{:S(2)}) copy-start(s32[8,4096]{1,0:T(8,128)} %samples_ref.3) | copy-start | bytes 393220
  33.7 4.0 %collective-permute-start = (bf16[16,64,128]{2,1,0:T(8,128)(2,1)S(1)}, bf16[16,64,128]{2,1,0:T(8,128)(2,1)S(1)}, u32[]{:S(2)}, u32[]{:S(2)}) collective-permute-start(bf16[16,64,128]{2,1,0:T(8,128)(2,1)S(1)} %all_to_all.16.after_ref.own_ref), channel_id=1, source_target_pairs={{0,1},{1,0},{2,3},{3,2},{4,5},{5,4},{6,7},{7,6},{8,9},{9,8},{10,11... | collective-permute-start | bytes 786440 | tf_op jit(solution)/shard_map/ppermute | solution.py:195

commit v6 on v5

--- a/solution.py
+++ b/solution.py
@@ -37,15 +37,16 @@
 
 
 def pack_kernel(state_ref, gates_ref, slot_ref, out_ref, slot_out_ref, held_ref, rows_ref, sems):
-    copies = [pltpu.make_async_copy(state_ref.at[c], held_ref.at[c], sems.at[c]) for c in range(Z)]
+    copies = [pltpu.make_async_copy(state_ref.at[c, i], held_ref.at[c, i], sems.at[2 * c + i]) for c in range(Z) for i in range(2)]
     for copy in copies:
         copy.start()
-    rows = pltpu.make_async_copy(gates_ref.at[:, mode_index()], rows_ref, sems.at[Z])
+    rows = pltpu.make_async_copy(gates_ref.at[:, mode_index()], rows_ref, sems.at[2 * Z])
     rows.start()
-    slots = pltpu.make_async_copy(slot_ref, slot_out_ref, sems.at[Z + 1])
+    slots = pltpu.make_async_copy(slot_ref, slot_out_ref, sems.at[2 * Z + 1])
     slots.start()
     for c in range(Z):
-        copies[c].wait()
+        copies[2 * c].wait()
+        copies[2 * c + 1].wait()
         for s in range(X):
             total = held_ref[c, 0, s].astype(F32) + held_ref[c, 1, s].astype(F32)
             out_ref[ZX_ORDER.index(c * X + s), 0:32, :] = total.astype(BF)
@@ -146,20 +147,31 @@
         out_ref[c, 32:40, :] = tail
 
 
-def finish_kernel(in_ref, held_ref, probs_ref, score_ref, amp_ref, wide_ref):
-    amp_ref[...] = held_ref[...]
+def finish_kernel(in_ref, held_ref, probs_ref, score_ref, amp_ref, wide_ref, done_ref, mean_ref, sems):
+    amps = pltpu.make_async_copy(held_ref, amp_ref, sems.at[4])
+    amps.start()
     for i, c in enumerate(Z_ORDER):
         tail = in_ref[i, 32:40, :].astype(F32)
         norm = tail[0:1] + tail[1:2]
         wide_ref[c * 32 : (c + 1) * 32, :] = in_ref[i, 0:32, :].astype(F32) * 65536.0 / norm
     total = jnp.zeros((Z, W), F32)
-    for j in range(32):
-        rows = wide_ref[pl.ds(j, Z, stride=32), :]
-        probs_ref[:, j * W : (j + 1) * W] = rows
-        total = total + rows
+    copies = []
+    for part in range(4):
+        for j in range(8 * part, 8 * part + 8):
+            rows = wide_ref[pl.ds(j, Z, stride=32), :]
+            done_ref[:, j * W : (j + 1) * W] = rows
+            total = total + rows
+        lanes = pl.ds(part * 1024, 1024)
+        copies.append(pltpu.make_async_copy(done_ref.at[:, lanes], probs_ref.at[:, lanes], sems.at[part]))
+        copies[-1].start()
     score = jnp.sum(total, axis=1, keepdims=True) * (1.0 / 4096.0)
     diag = lax.broadcasted_iota(I32, (Z, W), 0) == lax.broadcasted_iota(I32, (Z, W), 1)
-    score_ref[...] = jnp.sum(jnp.where(diag, score, 0.0), axis=0, keepdims=True)[:, :Z]
+    mean_ref[...] = jnp.sum(jnp.where(diag, score, 0.0), axis=0, keepdims=True)[:, :Z]
+    copies.append(pltpu.make_async_copy(mean_ref, score_ref, sems.at[5]))
+    copies[-1].start()
+    for copy in copies:
+        copy.wait()
+    amps.wait()
 
 
 def hbm(array):
@@ -178,7 +190,7 @@
         out_shape=(shape((Z * X, 40, W), BF), shape((1, Z * X), I32)),
         in_specs=[HB, HB, HB],
         out_specs=(VM, VM),
-        scratch_shapes=[pltpu.VMEM((Z, 2, X, 32, W), BF), pltpu.VMEM((X, 8, W), BF), pltpu.SemaphoreType.DMA((Z + 2,))],
+        scratch_shapes=[pltpu.VMEM((Z, 2, X, 32, W), BF), pltpu.VMEM((X, 8, W), BF), pltpu.SemaphoreType.DMA((2 * Z + 2,))],
         compiler_params=CP,
         name="pack",
     )(hbm(state), hbm(gate_blocks.reshape(X, M, 8, W)), hbm(gate_slot.reshape(1, Z * X)))
@@ -215,8 +227,8 @@
         finish_kernel,
         out_shape=(shape((Z, 4096), F32), shape((1, Z), F32), shape((1, 16, 2, W), F32)),
         in_specs=[VM, VM],
-        out_specs=(VM, VM, VM),
-        scratch_shapes=[pltpu.VMEM((Z * 32, W), F32)],
+        out_specs=(ANY, ANY, ANY),
+        scratch_shapes=[pltpu.VMEM((Z * 32, W), F32), pltpu.VMEM((Z, 4096), F32), pltpu.VMEM((1, Z), F32), pltpu.SemaphoreType.DMA((6,))],
         compiler_params=CP, name="finish",
     )(picked, amplitudes)
     return amplitudes, probs, score.reshape(Z)

time: 49.2 us -> 49.2 us (level)
  no operation moved by 1% of the time
where the time goes in v6:
time: 49.2 us; the launch traced here: 48.6 us
  blocking collectives  40.5 us (82%)
  Pallas kernels  3.73 us (8%)
  starting transfers between devices  2.79 us (6%)
  waiting for transfers between devices  0.91 us (2%)
  between operations  0.66 us (1%)
    all_to_all x3, blocking collectives, exchange(): lax.all_to_all(array, axes, split_axis=0, concat_axis=0, tiled=True, axis...  40.5 us
    ppermute x1, starting transfers between devices, on_device(): pair = lax.ppermute(plane, 'k', [(0, 1), (1, 0)])  2.79 us
    pallas_call x1, Pallas kernels, on_device(): pl.pallas_call(apply_kernel, out_shape=(shape((1, 16, 2, W), F32), shape(...  1.35 us
    pallas_call x1, Pallas kernels, on_device(): pl.pallas_call(pack_kernel, out_shape=(shape((Z * X, 40, W), BF), shape((...  1.21 us
  transfers between devices with their start and end apart: 1, of which 1 were waited for; matrix products, arithmetic and copies ran while one was open for 0% of the time, Pallas kernels for 1%

profile of v6, /device:TPU:1, one launch (start us, length us, event | category | flops | bytes accessed | tf_op | source)
XLA Modules:
  0.0 48.6 jit_solution(16401358663544969226)
XLA Ops:
  0.6 0.0 copy-start
  0.6 1.2 %pack.1 = (bf16[32,40,128]{2,1,0:T(8,128)(2,1)S(1)}, s32[1,32]{1,0:T(1,128)S(1)}) custom-call(bf16[8,2,4,32,128]{4,3,2,1,0:T(8,128)(2,1)} %bitcast.4, bf16[4,8,8,128]{3,2,1,0:T(8,128)(2,1)} %bitcast.5, s32[1,32]{1,0:T(1,128)} %bitcast.6), custom_call_target="tpu_custom_call" | custom-call | tf_op jit(solution)/shard_map/pack/pallas_call | solution.py:188
  1.9 21.5 %all_to_all.15.in_ref = bf16[32,40,128]{2,1,0:T(8,128)(2,1)S(1)} all-to-all(bf16[32,40,128]{2,1,0:T(8,128)(2,1)S(1)} %get-tuple-element.11), channel_id=1, replica_groups={{144,128,136,152,16,0,8,24,48,32,40,56,80,64,72,88,112,96,104,120,176,1..., dimensions={0} | all-to-all | bytes 655360 | tf_op jit(solution)/shard_map/all_to_all | solution.py:182
  23.3 0.1 sum.1
  23.5 10.2 %all_to_all.16.after_ref.own_ref = bf16[16,64,128]{2,1,0:T(8,128)(2,1)S(1)} all-to-all(bf16[16,64,128]{2,1,0:T(8,128)(2,1)S(1)} %sum.1), channel_id=1, replica_groups={{20,4,12,28,16,0,8,24,18,2,10,26,22,6,14,30},{21,5,13,29,17,1,9,25,19,3..., dimensions={0} | all-to-all | bytes 524288 | tf_op jit(solution)/shard_map/all_to_all | solution.py:182
  33.7 2.8 %collective-permute-start = (bf16[16,64,128]{2,1,0:T(8,128)(2,1)S(1)}, bf16[16,64,128]{2,1,0:T(8,128)(2,1)S(1)}, u32[]{:S(2)}, u32[]{:S(2)}) collective-permute-start(bf16[16,64,128]{2,1,0:T(8,128)(2,1)S(1)} %all_to_all.16.after_ref.own_ref), channel_id=1, source_target_pairs={{0,1},{1,0},{2,3},{3,2},{4,5},{5,4},{6,7},{7,6},{8,9},{9,8},{10,11... | collective-permute-start | bytes 786440 | tf_op jit(solution)/shard_map/ppermute | solution.py:207
  36.5 0.0 copy-done
  36.5 0.2 hot.1.hot_ref
  36.7 0.9 %collective-permute-done.pair_ref = bf16[16,64,128]{2,1,0:T(8,128)(2,1)S(1)} collective-permute-done((bf16[16,64,128]{2,1,0:T(8,128)(2,1)S(1)}, bf16[16,64,128]{2,1,0:T(8,128)(2,1)S(1)}, u32[]{:S(2)}, u32[]{:S(2)}) %collective-permute-start) | collective-permute-done | bytes 262176 | tf_op jit(solution)/shard_map/ppermute | solution.py:207
  37.6 1.4 %apply.1 = (f32[1,16,2,128]{3,2,1,0:T(2,128)S(1)}, bf16[8,40,128]{2,1,0:T(8,128)(2,1)S(1)}) custom-call(s32[8,4096]{1,0:T(8,128)S(1)} %copy-done, bf16[256,4096]{1,0:T(8,128)(2,1)S(1)} %hot.1.hot_ref, bf16[16,64,128]{2,1,0:T(8,128)(2,1)S(1)} %all_to_all.16.after_ref.own_ref, bf16[16,64,128]{2,1,0:T(8,128)(2,1)S(1)} %collective-permute-done.pair_ref), custom_call_target="tpu_custom_call" | custom-call | tf_op jit(solution)/shard_map/apply/pallas_call | solution.py:217
  39.0 8.8 %all_to_all.17.in_ref = bf16[8,40,128]{2,1,0:T(8,128)(2,1)S(1)} all-to-all(bf16[8,40,128]{2,1,0:T(8,128)(2,1)S(1)} %get-tuple-element.12), channel_id=1, replica_groups={{128,0,32,64,96,160,192,224},{129,1,33,65,97,161,193,225},{130,2,34,66,..., dimensions={0} | all-to-all | bytes 163840 | tf_op jit(solution)/shard_map/all_to_all | solution.py:182
  47.8 0.8 %finish.1 = (f32[8,4096]{1,0:T(8,128)}, f32[1,8]{1,0:T(1,128)}, f32[1,16,2,128]{3,2,1,0:T(2,128)}) custom-call(bf16[8,40,128]{2,1,0:T(8,128)(2,1)S(1)} %all_to_all.17.in_ref, f32[1,16,2,128]{3,2,1,0:T(2,128)S(1)} %get-tuple-element.13.held_ref), custom_call_target="tpu_custom_call" | custom-call | tf_op jit(solution)/shard_map/finish/pallas_call | solution.py:226
Async XLA Ops:
  0.6 35.8 %copy-start = (s32[8,4096]{1,0:T(8,128)S(1)}, s32[8,4096]{1,0:T(8,128)}, u32[]{:S(2)}) copy-start(s32[8,4096]{1,0:T(8,128)} %samples_ref.3) | copy-start | bytes 393220
  33.7 4.0 %collective-permute-start = (bf16[16,64,128]{2,1,0:T(8,128)(2,1)S(1)}, bf16[16,64,128]{2,1,0:T(8,128)(2,1)S(1)}, u32[]{:S(2)}, u32[]{:S(2)}) collective-permute-start(bf16[16,64,128]{2,1,0:T(8,128)(2,1)S(1)} %all_to_all.16.after_ref.own_ref), channel_id=1, source_target_pairs={{0,1},{1,0},{2,3},{3,2},{4,5},{5,4},{6,7},{7,6},{8,9},{9,8},{10,11... | collective-permute-start | bytes 786440 | tf_op jit(solution)/shard_map/ppermute | solution.py:207

commit v7 on v6

--- a/solution.py
+++ b/solution.py
@@ -23,6 +23,7 @@
     return [first] + [i for i in range(count) if i != first]
 
 
+Z_LAST = [4, 0, 7, 1, 6, 2, 5, 3]
 Z_ORDER, X_ORDER, Y_ORDER = led_by(Z_FIRST, Z), led_by(X_FIRST, X), led_by(Y_FIRST, Y)
 ZX_ORDER = [z * X + x for z in Z_ORDER for x in X_ORDER]
 XY_ORDER = [x * Y + y for y in Y_ORDER for x in X_ORDER]
@@ -150,7 +151,7 @@
 def finish_kernel(in_ref, held_ref, probs_ref, score_ref, amp_ref, wide_ref, done_ref, mean_ref, sems):
     amps = pltpu.make_async_copy(held_ref, amp_ref, sems.at[4])
     amps.start()
-    for i, c in enumerate(Z_ORDER):
+    for i, c in enumerate(Z_LAST):
         tail = in_ref[i, 32:40, :].astype(F32)
         norm = tail[0:1] + tail[1:2]
         wide_ref[c * 32 : (c + 1) * 32, :] = in_ref[i, 0:32, :].astype(F32) * 65536.0 / norm
@@ -222,7 +223,7 @@
         scratch_shapes=[pltpu.VMEM((X * Y, K, 64, W), BF), pltpu.VMEM((X, 2, W, W), F32), pltpu.VMEM((32, W), F32)],
         compiler_params=CP, name="apply",
     )(samples, hot, plane, pair)
-    picked = exchange(picked, "z", Z_ORDER)
+    picked = exchange(picked, "z", Z_LAST)
     probs, score, amplitudes = pl.pallas_call(
         finish_kernel,
         out_shape=(shape((Z, 4096), F32), shape((1, Z), F32), shape((1, 16, 2, W), F32)),

time: 49.2 us -> 49.2 us (level)
  no operation moved by 1% of the time
where the time goes in v7:
time: 49.2 us; the launch traced here: 48.7 us
  blocking collectives  40.6 us (83%)
  Pallas kernels  3.74 us (8%)
  starting transfers between devices  2.79 us (6%)
  waiting for transfers between devices  0.91 us (2%)
  between operations  0.66 us (1%)
    all_to_all x3, blocking collectives, exchange(): lax.all_to_all(array, axes, split_axis=0, concat_axis=0, tiled=True, axis...  40.6 us
    ppermute x1, starting transfers between devices, on_device(): pair = lax.ppermute(plane, 'k', [(0, 1), (1, 0)])  2.79 us
    pallas_call x1, Pallas kernels, on_device(): pl.pallas_call(apply_kernel, out_shape=(shape((1, 16, 2, W), F32), shape(...  1.35 us
    pallas_call x1, Pallas kernels, on_device(): pl.pallas_call(pack_kernel, out_shape=(shape((Z * X, 40, W), BF), shape((...  1.21 us
  transfers between devices with their start and end apart: 1, of which 1 were waited for; matrix products, arithmetic and copies ran while one was open for 0% of the time, Pallas kernels for 1%

profile of v7, /device:TPU:1, one launch (start us, length us, event | category | flops | bytes accessed | tf_op | source)
XLA Modules:
  0.0 48.7 jit_solution(9985021938057763596)
XLA Ops:
  0.6 0.0 copy-start
  0.6 1.2 %pack.1 = (bf16[32,40,128]{2,1,0:T(8,128)(2,1)S(1)}, s32[1,32]{1,0:T(1,128)S(1)}) custom-call(bf16[8,2,4,32,128]{4,3,2,1,0:T(8,128)(2,1)} %bitcast.4, bf16[4,8,8,128]{3,2,1,0:T(8,128)(2,1)} %bitcast.5, s32[1,32]{1,0:T(1,128)} %bitcast.6), custom_call_target="tpu_custom_call" | custom-call | tf_op jit(solution)/shard_map/pack/pallas_call | solution.py:189
  1.9 21.5 %all_to_all.15.in_ref = bf16[32,40,128]{2,1,0:T(8,128)(2,1)S(1)} all-to-all(bf16[32,40,128]{2,1,0:T(8,128)(2,1)S(1)} %get-tuple-element.11), channel_id=1, replica_groups={{144,128,136,152,16,0,8,24,48,32,40,56,80,64,72,88,112,96,104,120,176,1..., dimensions={0} | all-to-all | bytes 655360 | tf_op jit(solution)/shard_map/all_to_all | solution.py:183
  23.3 0.1 sum.1
  23.5 10.2 %all_to_all.16.after_ref.own_ref = bf16[16,64,128]{2,1,0:T(8,128)(2,1)S(1)} all-to-all(bf16[16,64,128]{2,1,0:T(8,128)(2,1)S(1)} %sum.1), channel_id=1, replica_groups={{20,4,12,28,16,0,8,24,18,2,10,26,22,6,14,30},{21,5,13,29,17,1,9,25,19,3..., dimensions={0} | all-to-all | bytes 524288 | tf_op jit(solution)/shard_map/all_to_all | solution.py:183
  33.7 2.8 %collective-permute-start = (bf16[16,64,128]{2,1,0:T(8,128)(2,1)S(1)}, bf16[16,64,128]{2,1,0:T(8,128)(2,1)S(1)}, u32[]{:S(2)}, u32[]{:S(2)}) collective-permute-start(bf16[16,64,128]{2,1,0:T(8,128)(2,1)S(1)} %all_to_all.16.after_ref.own_ref), channel_id=1, source_target_pairs={{0,1},{1,0},{2,3},{3,2},{4,5},{5,4},{6,7},{7,6},{8,9},{9,8},{10,11... | collective-permute-start | bytes 786440 | tf_op jit(solution)/shard_map/ppermute | solution.py:208
  36.5 0.0 copy-done
  36.5 0.2 hot.1.hot_ref
  36.7 0.9 %collective-permute-done.pair_ref = bf16[16,64,128]{2,1,0:T(8,128)(2,1)S(1)} collective-permute-done((bf16[16,64,128]{2,1,0:T(8,128)(2,1)S(1)}, bf16[16,64,128]{2,1,0:T(8,128)(2,1)S(1)}, u32[]{:S(2)}, u32[]{:S(2)}) %collective-permute-start) | collective-permute-done | bytes 262176 | tf_op jit(solution)/shard_map/ppermute | solution.py:208
  37.6 1.4 %apply.1 = (f32[1,16,2,128]{3,2,1,0:T(2,128)S(1)}, bf16[8,40,128]{2,1,0:T(8,128)(2,1)S(1)}) custom-call(s32[8,4096]{1,0:T(8,128)S(1)} %copy-done, bf16[256,4096]{1,0:T(8,128)(2,1)S(1)} %hot.1.hot_ref, bf16[16,64,128]{2,1,0:T(8,128)(2,1)S(1)} %all_to_all.16.after_ref.own_ref, bf16[16,64,128]{2,1,0:T(8,128)(2,1)S(1)} %collective-permute-done.pair_ref), custom_call_target="tpu_custom_call" | custom-call | tf_op jit(solution)/shard_map/apply/pallas_call | solution.py:218
  39.0 8.9 %all_to_all.17.in_ref = bf16[8,40,128]{2,1,0:T(8,128)(2,1)S(1)} all-to-all(bf16[8,40,128]{2,1,0:T(8,128)(2,1)S(1)} %get-tuple-element.12), channel_id=1, replica_groups={{128,0,224,32,192,64,160,96},{129,1,225,33,193,65,161,97},{130,2,226,34..., dimensions={0} | all-to-all | bytes 163840 | tf_op jit(solution)/shard_map/all_to_all | solution.py:183
  47.9 0.8 %finish.1 = (f32[8,4096]{1,0:T(8,128)}, f32[1,8]{1,0:T(1,128)}, f32[1,16,2,128]{3,2,1,0:T(2,128)}) custom-call(bf16[8,40,128]{2,1,0:T(8,128)(2,1)S(1)} %all_to_all.17.in_ref, f32[1,16,2,128]{3,2,1,0:T(2,128)S(1)} %get-tuple-element.13.held_ref), custom_call_target="tpu_custom_call" | custom-call | tf_op jit(solution)/shard_map/finish/pallas_call | solution.py:227
Async XLA Ops:
  0.6 35.8 %copy-start = (s32[8,4096]{1,0:T(8,128)S(1)}, s32[8,4096]{1,0:T(8,128)}, u32[]{:S(2)}) copy-start(s32[8,4096]{1,0:T(8,128)} %samples_ref.3) | copy-start | bytes 393220
  33.7 4.0 %collective-permute-start = (bf16[16,64,128]{2,1,0:T(8,128)(2,1)S(1)}, bf16[16,64,128]{2,1,0:T(8,128)(2,1)S(1)}, u32[]{:S(2)}, u32[]{:S(2)}) collective-permute-start(bf16[16,64,128]{2,1,0:T(8,128)(2,1)S(1)} %all_to_all.16.after_ref.own_ref), channel_id=1, source_target_pairs={{0,1},{1,0},{2,3},{3,2},{4,5},{5,4},{6,7},{7,6},{8,9},{9,8},{10,11... | collective-permute-start | bytes 786440 | tf_op jit(solution)/shard_map/ppermute | solution.py:208

commit v8 on v5

--- a/solution.py
+++ b/solution.py
@@ -37,15 +37,16 @@
 
 
 def pack_kernel(state_ref, gates_ref, slot_ref, out_ref, slot_out_ref, held_ref, rows_ref, sems):
-    copies = [pltpu.make_async_copy(state_ref.at[c], held_ref.at[c], sems.at[c]) for c in range(Z)]
+    copies = [pltpu.make_async_copy(state_ref.at[c, i], held_ref.at[c, i], sems.at[2 * c + i]) for c in range(Z) for i in range(2)]
     for copy in copies:
         copy.start()
-    rows = pltpu.make_async_copy(gates_ref.at[:, mode_index()], rows_ref, sems.at[Z])
+    rows = pltpu.make_async_copy(gates_ref.at[:, mode_index()], rows_ref, sems.at[2 * Z])
     rows.start()
-    slots = pltpu.make_async_copy(slot_ref, slot_out_ref, sems.at[Z + 1])
+    slots = pltpu.make_async_copy(slot_ref, slot_out_ref, sems.at[2 * Z + 1])
     slots.start()
     for c in range(Z):
-        copies[c].wait()
+        copies[2 * c].wait()
+        copies[2 * c + 1].wait()
         for s in range(X):
             total = held_ref[c, 0, s].astype(F32) + held_ref[c, 1, s].astype(F32)
             out_ref[ZX_ORDER.index(c * X + s), 0:32, :] = total.astype(BF)
@@ -178,7 +179,7 @@
         out_shape=(shape((Z * X, 40, W), BF), shape((1, Z * X), I32)),
         in_specs=[HB, HB, HB],
         out_specs=(VM, VM),
-        scratch_shapes=[pltpu.VMEM((Z, 2, X, 32, W), BF), pltpu.VMEM((X, 8, W), BF), pltpu.SemaphoreType.DMA((Z + 2,))],
+        scratch_shapes=[pltpu.VMEM((Z, 2, X, 32, W), BF), pltpu.VMEM((X, 8, W), BF), pltpu.SemaphoreType.DMA((2 * Z + 2,))],
         compiler_params=CP,
         name="pack",
     )(hbm(state), hbm(gate_blocks.reshape(X, M, 8, W)), hbm(gate_slot.reshape(1, Z * X)))

time: 49.2 us -> 49.2 us (level)
  no operation moved by 1% of the time
where the time goes in v8:
time: 49.2 us; the launch traced here: 48.6 us
  blocking collectives  40.5 us (82%)
  Pallas kernels  3.74 us (8%)
  starting transfers between devices  2.79 us (6%)
  waiting for transfers between devices  0.91 us (2%)
  between operations  0.66 us (1%)
    all_to_all x3, blocking collectives, exchange(): lax.all_to_all(array, axes, split_axis=0, concat_axis=0, tiled=True, axis...  40.5 us
    ppermute x1, starting transfers between devices, on_device(): pair = lax.ppermute(plane, 'k', [(0, 1), (1, 0)])  2.79 us
    pallas_call x1, Pallas kernels, on_device(): pl.pallas_call(apply_kernel, out_shape=(shape((1, 16, 2, W), F32), shape(...  1.35 us
    pallas_call x1, Pallas kernels, on_device(): pl.pallas_call(pack_kernel, out_shape=(shape((Z * X, 40, W), BF), shape((...  1.21 us
  transfers between devices with their start and end apart: 1, of which 1 were waited for; matrix products, arithmetic and copies ran while one was open for 0% of the time, Pallas kernels for 1%

profile of v8, /device:TPU:1, one launch (start us, length us, event | category | flops | bytes accessed | tf_op | source)
XLA Modules:
  0.0 48.6 jit_solution(7075764544376323095)
XLA Ops:
  0.6 0.0 copy-start
  0.6 1.2 %pack.1 = (bf16[32,40,128]{2,1,0:T(8,128)(2,1)S(1)}, s32[1,32]{1,0:T(1,128)S(1)}) custom-call(bf16[8,2,4,32,128]{4,3,2,1,0:T(8,128)(2,1)} %bitcast.4, bf16[4,8,8,128]{3,2,1,0:T(8,128)(2,1)} %bitcast.5, s32[1,32]{1,0:T(1,128)} %bitcast.6), custom_call_target="tpu_custom_call" | custom-call | tf_op jit(solution)/shard_map/pack/pallas_call | solution.py:177
  1.9 21.5 %all_to_all.15.in_ref = bf16[32,40,128]{2,1,0:T(8,128)(2,1)S(1)} all-to-all(bf16[32,40,128]{2,1,0:T(8,128)(2,1)S(1)} %get-tuple-element.11), channel_id=1, replica_groups={{144,128,136,152,16,0,8,24,48,32,40,56,80,64,72,88,112,96,104,120,176,1..., dimensions={0} | all-to-all | bytes 655360 | tf_op jit(solution)/shard_map/all_to_all | solution.py:171
  23.3 0.1 sum.1
  23.5 10.2 %all_to_all.16.after_ref.own_ref = bf16[16,64,128]{2,1,0:T(8,128)(2,1)S(1)} all-to-all(bf16[16,64,128]{2,1,0:T(8,128)(2,1)S(1)} %sum.1), channel_id=1, replica_groups={{20,4,12,28,16,0,8,24,18,2,10,26,22,6,14,30},{21,5,13,29,17,1,9,25,19,3..., dimensions={0} | all-to-all | bytes 524288 | tf_op jit(solution)/shard_map/all_to_all | solution.py:171
  33.7 2.8 %collective-permute-start = (bf16[16,64,128]{2,1,0:T(8,128)(2,1)S(1)}, bf16[16,64,128]{2,1,0:T(8,128)(2,1)S(1)}, u32[]{:S(2)}, u32[]{:S(2)}) collective-permute-start(bf16[16,64,128]{2,1,0:T(8,128)(2,1)S(1)} %all_to_all.16.after_ref.own_ref), channel_id=1, source_target_pairs={{0,1},{1,0},{2,3},{3,2},{4,5},{5,4},{6,7},{7,6},{8,9},{9,8},{10,11... | collective-permute-start | bytes 786440 | tf_op jit(solution)/shard_map/ppermute | solution.py:196
  36.5 0.0 copy-done
  36.5 0.2 hot.1.hot_ref
  36.7 0.9 %collective-permute-done.pair_ref = bf16[16,64,128]{2,1,0:T(8,128)(2,1)S(1)} collective-permute-done((bf16[16,64,128]{2,1,0:T(8,128)(2,1)S(1)}, bf16[16,64,128]{2,1,0:T(8,128)(2,1)S(1)}, u32[]{:S(2)}, u32[]{:S(2)}) %collective-permute-start) | collective-permute-done | bytes 262176 | tf_op jit(solution)/shard_map/ppermute | solution.py:196
  37.6 1.4 %apply.1 = (f32[1,16,2,128]{3,2,1,0:T(2,128)S(1)}, bf16[8,40,128]{2,1,0:T(8,128)(2,1)S(1)}) custom-call(s32[8,4096]{1,0:T(8,128)S(1)} %copy-done, bf16[256,4096]{1,0:T(8,128)(2,1)S(1)} %hot.1.hot_ref, bf16[16,64,128]{2,1,0:T(8,128)(2,1)S(1)} %all_to_all.16.after_ref.own_ref, bf16[16,64,128]{2,1,0:T(8,128)(2,1)S(1)} %collective-permute-done.pair_ref), custom_call_target="tpu_custom_call" | custom-call | tf_op jit(solution)/shard_map/apply/pallas_call | solution.py:206
  39.0 8.8 %all_to_all.17.in_ref = bf16[8,40,128]{2,1,0:T(8,128)(2,1)S(1)} all-to-all(bf16[8,40,128]{2,1,0:T(8,128)(2,1)S(1)} %get-tuple-element.12), channel_id=1, replica_groups={{128,0,32,64,96,160,192,224},{129,1,33,65,97,161,193,225},{130,2,34,66,..., dimensions={0} | all-to-all | bytes 163840 | tf_op jit(solution)/shard_map/all_to_all | solution.py:171
  47.8 0.8 %finish.1 = (f32[8,4096]{1,0:T(8,128)}, f32[1,8]{1,0:T(1,128)}, f32[1,16,2,128]{3,2,1,0:T(2,128)}) custom-call(bf16[8,40,128]{2,1,0:T(8,128)(2,1)S(1)} %all_to_all.17.in_ref, f32[1,16,2,128]{3,2,1,0:T(2,128)S(1)} %get-tuple-element.13.held_ref), custom_call_target="tpu_custom_call" | custom-call | tf_op jit(solution)/shard_map/finish/pallas_call | solution.py:215
Async XLA Ops:
  0.6 35.8 %copy-start = (s32[8,4096]{1,0:T(8,128)S(1)}, s32[8,4096]{1,0:T(8,128)}, u32[]{:S(2)}) copy-start(s32[8,4096]{1,0:T(8,128)} %samples_ref.3) | copy-start | bytes 393220
  33.7 4.0 %collective-permute-start = (bf16[16,64,128]{2,1,0:T(8,128)(2,1)S(1)}, bf16[16,64,128]{2,1,0:T(8,128)(2,1)S(1)}, u32[]{:S(2)}, u32[]{:S(2)}) collective-permute-start(bf16[16,64,128]{2,1,0:T(8,128)(2,1)S(1)} %all_to_all.16.after_ref.own_ref), channel_id=1, source_target_pairs={{0,1},{1,0},{2,3},{3,2},{4,5},{5,4},{6,7},{7,6},{8,9},{9,8},{10,11... | collective-permute-start | bytes 786440 | tf_op jit(solution)/shard_map/ppermute | solution.py:196
